TPU v7x, 256 devices: a whole 4x4x8 slice. The times are simulated.
256 devices in a mesh: dp: 32 (over y, z), group: 8 (over x, core).
Axes of the slice: x: 4, y: 4, z: 8, core: 2. Of those that a mesh axis runs over, the one named last changes fastest.
Arguments:
- rewards: bfloat16 [65536, 4096], P(('dp', 'group')), may hold values from -6 to 6
- values: bfloat16 [65536, 4096], P(('dp', 'group')), may hold values from -6 to 6
- lengths: int32 [65536], P(('dp', 'group')), may hold values from 1 to 4096
- decay_rate: float32 [65536], P(('dp', 'group')), may hold values from 3.8146973e-06 to 0.03125
- piece_dest: int32 [32, 32], P('dp'), may hold values from 0 to 31, each once within a row
- row_perm: int32 [512, 128], P(('dp', 'group')), may hold values from 0 to 127, each once within a row
- minibatch: int32 [65536], P(('dp', 'group')), may hold values from 0 to 63
Outputs:
- white_rewards: bfloat16 [65536, 4096], P(('dp', 'group'))
- white_advantage: bfloat16 [65536, 4096], P(('dp', 'group'))
Inputs may be any that keep to these rules, and one draw needn't show every extreme that they name: Each row of piece_dest names every index of dp once. Each row of row_perm names every number below 128 once.
All inputs are finite; a program needn't handle non-finite values.
Results may differ from a plain program's by a relative error of at most 0.0049.
Values may be sent and summed in bfloat16 or wider, within the bound.
A program may use at most 64 MiB of HBM per device.

v0:
```python
import jax
import jax.numpy as jnp
from jax import lax
from jax.sharding import Mesh
from jax.sharding import PartitionSpec as P

MINIBATCHES = 64
DP_GROUP = ("dp_0", "dp_1", "group_0", "group_1")
DP = ("dp_0", "dp_1")


HIGHEST = lax.Precision.HIGHEST


def over_axes(value, axes):
    for axis in axes:
        value = lax.psum(value, axis)
    return value


def discounted(rewards, values, lengths, decay_rate):
    rows_here, span = rewards.shape
    block = min(128, span)
    blocks_here = span // block
    position = jnp.arange(span, dtype=jnp.int32)
    is_valid = position[None, :] < lengths[:, None]
    next_valid = position[None, :] + 1 < lengths[:, None]
    per_step = jnp.exp(-decay_rate)
    value_f = values.astype(jnp.float32)
    value_next = jnp.concatenate([value_f[:, 1:], jnp.zeros((rows_here, 1), jnp.float32)], axis=1)
    td_error = (
        rewards.astype(jnp.float32)
        + per_step[:, None] * jnp.where(next_valid, value_next, 0.0)
        - value_f
    )
    td_error = jnp.where(is_valid, td_error, 0.0).reshape(rows_here, blocks_here, block)
    offset = jnp.arange(block, dtype=jnp.float32)
    lower_scale = jnp.exp(-decay_rate[:, None] * offset[None, :])
    upper_scale = jnp.exp(decay_rate[:, None] * offset[None, :])
    triangle = (offset[:, None] >= offset[None, :]).astype(jnp.float32)
    scaled = td_error * lower_scale[:, None, :]
    summed = jnp.einsum("rjk,kt->rjt", scaled, triangle, precision=HIGHEST)
    local_part = summed * upper_scale[:, None, :]
    heads = local_part[:, :, 0]
    block_step = jnp.exp(-decay_rate * block)

    def carry_step(carry, head):
        fresh = head + block_step * carry
        return (fresh, fresh)

    final_carry, starts = lax.scan(carry_step, jnp.zeros_like(decay_rate), heads.T, reverse=True)
    next_heads = jnp.concatenate([starts[1:].T, jnp.zeros((rows_here, 1), jnp.float32)], axis=1)
    reach = jnp.exp(-decay_rate[:, None] * (block - offset[None, :]))
    total = local_part + reach[:, None, :] * next_heads[:, :, None]
    return jnp.where(is_valid, total.reshape(rows_here, span), 0.0).astype(jnp.bfloat16)


def by_target(array, piece_dest):
    peers = piece_dest.shape[1]
    target = piece_dest[0]
    slots = jnp.arange(peers, dtype=jnp.int32)
    source_slot = jnp.sum(jnp.where(target[None, :] == slots[:, None], slots[None, :], 0), axis=1)
    pieces = array.reshape((peers, array.shape[0] // peers) + array.shape[1:])
    return jnp.take(pieces, source_slot, axis=0).reshape(array.shape)


def reorder(received, row_perm):
    blocks_here, block = row_perm.shape
    chooser = (row_perm[:, :, None] == jnp.arange(block, dtype=jnp.int32)[None, None, :]).astype(
        jnp.bfloat16
    )

    def permute_one(member):
        shaped = member.reshape(blocks_here, block, member.shape[-1])
        mixed = jnp.einsum("bim,bmc->bic", chooser, shaped, preferred_element_type=jnp.float32)
        return mixed.astype(jnp.bfloat16).reshape(member.shape)

    return tuple((permute_one(member) for member in received))


def whiten(rewards, advantage, lengths, minibatch):
    rows_here, span = rewards.shape
    position = jnp.arange(span, dtype=jnp.int32)
    is_valid = position[None, :] < lengths[:, None]
    counted = lengths.astype(jnp.float32)
    reward_f = jnp.where(is_valid, rewards.astype(jnp.float32), 0.0)
    advantage_f = jnp.where(is_valid, advantage.astype(jnp.float32), 0.0)
    member = (minibatch[:, None] == jnp.arange(MINIBATCHES, dtype=jnp.int32)[None, :]).astype(
        jnp.float32
    )
    row_terms = jnp.stack(
        [
            counted,
            jnp.sum(reward_f, axis=1),
            jnp.sum(advantage_f, axis=1),
            jnp.sum(reward_f * reward_f, axis=1),
            jnp.sum(advantage_f * advantage_f, axis=1),
        ],
        axis=1,
    )
    totals = over_axes(jnp.dot(member.T, row_terms, precision=HIGHEST), DP_GROUP)
    count = jnp.maximum(totals[:, 0], 1.0)
    means = totals[:, 1:3] / count[:, None]
    spreads = totals[:, 3:5] / count[:, None] - means * means
    row_means = jnp.dot(member, means, precision=HIGHEST)
    row_scale = jnp.dot(member, lax.rsqrt(spreads + 1e-05), precision=HIGHEST)
    white_rewards = jnp.where(is_valid, (reward_f - row_means[:, 0:1]) * row_scale[:, 0:1], 0.0)
    white_advantage = jnp.where(
        is_valid, (advantage_f - row_means[:, 1:2]) * row_scale[:, 1:2], 0.0
    )
    return (white_rewards.astype(jnp.bfloat16), white_advantage.astype(jnp.bfloat16))


def local(rewards, values, lengths, decay_rate, piece_dest, row_perm, minibatch):
    blocks_here, block = row_perm.shape
    new_order = (jnp.arange(blocks_here, dtype=jnp.int32)[:, None] * block + row_perm).reshape(-1)
    per_row = jnp.stack([lengths.astype(jnp.float32), decay_rate], axis=1)
    moved_terms = lax.all_to_all(
        by_target(per_row, piece_dest), DP, split_axis=0, concat_axis=0, tiled=True
    )
    moved_terms = jnp.take(moved_terms, new_order, axis=0)
    lengths_here = moved_terms[:, 0].astype(jnp.int32)
    rate_here = moved_terms[:, 1]
    moved_rewards, moved_second = reorder(
        (
            lax.all_to_all(
                by_target(rewards, piece_dest), DP, split_axis=0, concat_axis=0, tiled=True
            ),
            lax.all_to_all(
                by_target(values, piece_dest), DP, split_axis=0, concat_axis=0, tiled=True
            ),
        ),
        row_perm,
    )
    advantage = discounted(moved_rewards, moved_second, lengths_here, rate_here)
    return whiten(moved_rewards, advantage, lengths_here, minibatch)


def solution(mesh):
    finer = Mesh(mesh.devices.reshape(4, 8, 4, 2), ("dp_0", "dp_1", "group_0", "group_1"))
    placed = (
        P(DP_GROUP, None),
        P(DP_GROUP, None),
        P(DP_GROUP),
        P(DP_GROUP),
        P(DP, None),
        P(DP_GROUP, None),
        P(DP_GROUP),
    )
    return jax.shard_map(
        local,
        mesh=finer,
        in_specs=placed,
        out_specs=(P(DP_GROUP, None), P(DP_GROUP, None)),
        check_vma=False,
    )
```

profile of v0, /device:TPU:1, one launch (start us, length us, event | category | flops | bytes accessed | tf_op | source)
XLA Modules:
  0.0 210.3 jit_solution(3992248455712595263)
XLA Ops:
  0.6 0.0 copy-start
  0.6 0.9 select_reduce_fusion
  1.6 0.7 convert_element_type.58
  2.3 0.1 stack.25
  2.4 0.8 stack.26
  3.2 0.6 gather_fusion
  3.8 0.7 broadcast_select_fusion.3
  4.5 12.0 %all-to-all-start = ((f32[32,8,2]{1,2,0:T(2,128)}), f32[32,8,2]{1,2,0:T(2,128)S(1)}, u32[]{:S(2)}, u32[]{:S(2)}) async-start(f32[32,8,2]{1,2,0:T(2,128)} %broadcast_select_fusion.3), calls=%async_computation | async-start | bytes 65536 | tf_op jit(solution)/shard_map/all_to_all | solution.py:118
  16.6 0.0 copy-done
  16.6 2.0 gather_fusion.2
  18.6 3.6 %gather_fusion.3 = bf16[32,8,4096]{2,1,0:T(8,128)(2,1)} fusion(bf16[32,8,4096]{2,1,0:T(8,128)(2,1)} %bitcast.80, s32[1024]{0:T(1024)S(1)} %pad_clamp_fusion), kind=kCustom, calls=%fused_computation.1.clone | custom fusion | bytes 4194432 | tf_op jit(solution)/shard_map/jit(_take)/gather | solution.py:64
  22.1 4.7 %broadcast_select_fusion = (bf16[32,8,4096]{2,1,0:T(8,128)(2,1)}, bf16[32,8,4096]{2,1,0:T(8,128)(2,1)}) fusion(bf16[32,8,4096]{2,1,0:T(8,128)(2,1)} %gather_fusion.3, pred[32]{0:T(512)(128)(4,1)S(1)} %compare_and_fusion, bf16[32,8,4096]{2,1,0:T(8,128)(2,1)} %gather_fusion.2), kind=kLoop, calls=%fused_computation.37 | loop fusion | flops 2097152 | bytes 8388640 | tf_op jit(solution)/shard_map/jit(_take)/select_n | solution.py:64
  26.8 0.0 all-to-all-done
  26.8 57.1 %all_to_all.21 = bf16[32,8,4096]{2,1,0:T(8,128)(2,1)} all-to-all(bf16[32,8,4096]{2,1,0:T(8,128)(2,1)} %get-tuple-element.154), channel_id=1, replica_groups=mesh['dp_0'=4,'dp_1'=8,'group_0'=4,'group_1'=2] {'dp_0','dp_1'}, dimensions={0} | all-to-all | bytes 4194304 | tf_op jit(solution)/shard_map/all_to_all | solution.py:129
  83.9 8.2 %all-to-all-start.1 = ((bf16[32,8,4096]{2,1,0:T(8,128)(2,1)}), bf16[32,8,4096]{2,1,0:T(8,128)(2,1)}, u32[]{:S(2)}, u32[]{:S(2)}) async-start(bf16[32,8,4096]{2,1,0:T(8,128)(2,1)} %get-tuple-element.155), calls=%async_computation.1 | async-start | bytes 4194304 | tf_op jit(solution)/shard_map/all_to_all | solution.py:126
  92.1 0.0 copy-done.6
  92.1 0.1 compare_and_fusion.1
  92.3 0.3 copy.57
  92.5 0.7 gather_fusion.1
  93.2 0.1 broadcast_select_fusion.2
  93.4 0.3 fusion.21
  93.6 0.1 multiply_exponential_fusion
  93.7 0.1 copy.53
  93.8 0.1 copy.55
  93.9 0.1 fusion.20
  94.0 2.3 %convolution_convert_fusion = bf16[2,128,4096]{2,1,0:T(8,128)(2,1)S(1)} fusion(bf16[2,128,4096]{2,1,0:T(8,128)(2,1)} %bitcast.78, s32[2,128]{1,0:T(2,128)S(1)} %copy-done.6), kind=kOutput, calls=%fused_computation.9 | convolution fusion | flops 269516800 | bytes 4195328 | tf_op jit(solution)/shard_map/bim,bmc->bic/dot_general | solution.py:75
  96.4 0.0 copy-start.1
  96.4 1.3 copy-done.1
  97.7 0.6 bitcast_convert_fusion
  98.3 3.1 %slice.58 = f32[256,4095]{1,0:T(8,128)} slice(f32[256,4096]{1,0:T(8,128)S(1)} %bitcast_convert_fusion), slice={[0:256], [1:4096]} | slice | bytes 8386560 | tf_op jit(solution)/shard_map/slice | solution.py:30
  101.5 39.4 %all-to-all-done.1 = bf16[32,8,4096]{2,1,0:T(8,128)(2,1)} async-done(((bf16[32,8,4096]{2,1,0:T(8,128)(2,1)}), bf16[32,8,4096]{2,1,0:T(8,128)(2,1)}, u32[]{:S(2)}, u32[]{:S(2)}) %all-to-all-start.1) | async-done | bytes 2097184 | tf_op jit(solution)/shard_map/all_to_all | solution.py:126
  140.9 3.0 %multiply_reduce_fusion.1 = (f32[2,128]{1,0:T(2,128)S(1)}, f32[2,128]{1,0:T(2,128)S(1)}, f32[2,128,4096]{2,1,0:T(8,128)S(1)}) fusion(s32[2,128]{1,0:T(2,128)S(1)} %bitcast.86, bf16[2,128,4096]{2,1,0:T(8,128)(2,1)} %bitcast.10, s32[2,128]{1,0:T(2,128)S(1)} %copy-done.6), kind=kOutput, calls=%fused_computation.27 | convolution fusion | flops 275807744 | bytes 6295552 | tf_op jit(solution)/shard_map/bim,bmc->bic/dot_general | solution.py:75
  143.9 0.4 copy-done.5
  144.3 1.8 fusion.10
  146.2 2.9 %fusion.14 = f32[256,32,128]{0,2,1:T(8,128)S(1)} fusion(f32[256,128]{0,1:T(8,128)S(1)} %get-tuple-element.157, f32[256,128]{1,0:T(8,128)S(1)} %copy.53, f32[256,4096]{1,0:T(8,128)S(1)} %fusion.10), kind=kOutput, calls=%fused_computation.34 | convolution fusion | flops 1612726272 | bytes 8650752 | tf_op jit(solution)/shard_map/rjk,kt->rjt/dot_general | solution.py:42
  149.0 2.0 copy-done.3
  151.1 3.3 %while.17 = (s32[]{:T(128)}, f32[256]{0:T(256)S(1)}, f32[32,256]{1,0:T(8,128)S(1)}, f32[32,256]{1,0:T(8,128)S(1)}, f32[256]{0:T(256)S(1)}, /*index=5*/s32[]{:T(128)}, s32[]{:T(128)}, s32[]{:T(128)}) while((s32[]{:T(128)}, f32[256]{0:T(256)S(1)}, f32[32,256]{1,0:T(8,128)S(1)}, f32[32,256]{1,0:T(8,128)S(1)}, f32[256]{0:T(256)S(1)}, ...), condition=%wide.region_3.5_spmd.clone, body=%wide.region_2.4_spmd.clone.sunk | while | flops 772 | bytes 8307 | solution.py:51
  154.4 5.0 %multiply_reduce_fusion = (f32[256]{0:T(256)S(1)}, f32[256]{0:T(256)S(1)}, bf16[256,32,128]{0,2,1:T(8,128)(2,1)}) fusion(s32[256]{0:T(256)S(1)} %fusion.20, s32[32,128]{1,0:T(8,128)S(1)} %multiply_add_fusion.1, f32[256,32,128]{0,2,1:T(8,128)} %copy-done.3, f32[256,32]{0,1:T(8,128)S(1)} %concatenate.8, f32[256,128]{0,1:T(8,128)S(1)} %get-tuple-element.152), kind=kLoop, calls=%fused_computation.26 | loop fusion | flops 10485248 | bytes 6474752 | tf_op jit(solution)/shard_map/reduce_sum | solution.py:97
  159.4 0.2 fusion.18
  159.6 6.5 %psum.28 = f32[64,5]{0,1:T(8,128)S(1)} all-reduce(f32[64,5]{0,1:T(8,128)S(1)} %fusion.18), channel_id=1, replica_groups=mesh['dp_0'=4,'dp_1'=8,'group_0'=4,'group_1'=2] {'dp_0'}, use_global_device_ids=true, to_apply=%region_7.9 | all-reduce | flops 320 | bytes 2560 | tf_op jit(solution)/shard_map/psum | solution.py:17
  166.1 14.4 %psum.29 = f32[64,5]{0,1:T(8,128)S(1)} all-reduce(f32[64,5]{0,1:T(8,128)S(1)} %psum.28), channel_id=1, replica_groups=mesh['dp_0'=4,'dp_1'=8,'group_0'=4,'group_1'=2] {'dp_1'}, use_global_device_ids=true, to_apply=%region_8.10 | all-reduce | flops 320 | bytes 2560 | tf_op jit(solution)/shard_map/psum | solution.py:17
  180.6 8.5 %psum.30 = f32[64,5]{0,1:T(8,128)S(1)} all-reduce(f32[64,5]{0,1:T(8,128)S(1)} %psum.29), channel_id=1, replica_groups=mesh['dp_0'=4,'dp_1'=8,'group_0'=4,'group_1'=2] {'group_0'}, use_global_device_ids=true, to_apply=%region_9.11 | all-reduce | flops 320 | bytes 2560 | tf_op jit(solution)/shard_map/psum | solution.py:17
  189.0 10.8 %psum.31 = f32[64,5]{0,1:T(8,128)S(1)} all-reduce(f32[64,5]{0,1:T(8,128)S(1)} %psum.30), channel_id=1, replica_groups=mesh['dp_0'=4,'dp_1'=8,'group_0'=4,'group_1'=2] {'group_1'}, use_global_device_ids=true, to_apply=%region_10.12 | all-reduce | flops 320 | bytes 2560 | tf_op jit(solution)/shard_map/psum | solution.py:17
  199.8 0.2 fusion.17
  200.0 0.3 fusion.16
  200.3 0.1 fusion.37
  200.3 4.1 %copy.56 = bf16[256,4096]{1,0:T(8,128)(2,1)} copy(bf16[256,4096]{0,1:T(8,128)(2,1)} %bitcast.79) | data formatting | bytes 4194304 | tf_op jit(solution)/shard_map/reshape | solution.py:55
  204.4 5.9 %select_convert_fusion = (bf16[256,4096]{1,0:T(8,128)(2,1)}, bf16[256,4096]{1,0:T(8,128)(2,1)}) fusion(bf16[256,4096]{1,0:T(8,128)(2,1)} %copy.56, f32[256]{0:T(256)S(1)} %bitcast.89, f32[256]{0:T(256)S(1)} %bitcast.87, s32[256]{0:T(256)S(1)} %fusion.20, f32[256]{0:T(256)S(1)} %bitcast.90, f32[256]{0:T(256)S(1)} %bitcast.88, f32[2,128,4096]{2,1,0:T(8,128)} %copy-done.4), kind=kLoop, calls=%fused_computation.24 | loop fusion | flops 13631488 | bytes 10490880 | tf_op jit(solution)/shard_map/convert_element_type | solution.py:111
  (127 shorter events, 2.4 us)
Async XLA Ops:
  0.6 15.9 %copy-start = (bf16[256,4096]{1,0:T(8,128)(2,1)S(1)}, bf16[256,4096]{1,0:T(8,128)(2,1)}, u32[]{:S(2)}) copy-start(bf16[256,4096]{1,0:T(8,128)(2,1)} %param.11) | copy-start | bytes 6291460
  4.5 22.3 %all-to-all-start = ((f32[32,8,2]{1,2,0:T(2,128)}), f32[32,8,2]{1,2,0:T(2,128)S(1)}, u32[]{:S(2)}, u32[]{:S(2)}) async-start(f32[32,8,2]{1,2,0:T(2,128)} %broadcast_select_fusion.3), calls=%async_computation | async-start | bytes 65536 | tf_op jit(solution)/shard_map/all_to_all | solution.py:118
  26.8 65.3 %copy-start.6 = (s32[2,128]{1,0:T(2,128)S(1)}, s32[2,128]{1,0:T(2,128)}, u32[]{:S(2)}) copy-start(s32[2,128]{1,0:T(2,128)} %param.16) | copy-start | bytes 3076
  83.9 56.9 %all-to-all-start.1 = ((bf16[32,8,4096]{2,1,0:T(8,128)(2,1)}), bf16[32,8,4096]{2,1,0:T(8,128)(2,1)}, u32[]{:S(2)}, u32[]{:S(2)}) async-start(bf16[32,8,4096]{2,1,0:T(8,128)(2,1)} %get-tuple-element.155), calls=%async_computation.1 | async-start | bytes 4194304 | tf_op jit(solution)/shard_map/all_to_all | solution.py:126
  96.4 1.3 copy-start.1
  140.9 3.0 %copy-start.2 = (bf16[2,128,4096]{2,1,0:T(8,128)(2,1)S(1)}, bf16[2,128,4096]{2,1,0:T(8,128)(2,1)}, u32[]{:S(2)}) copy-start(bf16[2,128,4096]{2,1,0:T(8,128)(2,1)} %copy-done.1) | copy-start | bytes 6291460
  140.9 3.5 %copy-start.5 = (f32[256,4095]{1,0:T(8,128)S(1)}, f32[256,4095]{1,0:T(8,128)}, u32[]{:S(2)}) copy-start(f32[256,4095]{1,0:T(8,128)} %slice.58) | copy-start | bytes 12579844
  143.9 2.2 %copy-start.4 = (f32[2,128,4096]{2,1,0:T(8,128)}, f32[2,128,4096]{2,1,0:T(8,128)S(1)}, u32[]{:S(2)}) copy-start(f32[2,128,4096]{2,1,0:T(8,128)S(1)} %get-tuple-element.156) | copy-start | bytes 12582916
  149.0 2.0 copy-start.3
  151.0 8.4 %copy-start.7 = (s32[256]{0:T(256)S(1)}, s32[256]{0:T(256)}, u32[]{:S(2)}) copy-start(s32[256]{0:T(256)} %param.17) | copy-start | bytes 3076
where the time goes:
time: 211 us; the launch traced here: 210 us
  blocking collectives  97.3 us (46%)
  waiting for transfers between devices  39.4 us (19%)
  other arithmetic  21.6 us (10%)
  local copies, waits for them, and re-layouts  21 us (10%)
  starting transfers between devices  20.2 us (10%)
  matrix products  8.92 us (4%)
    all_to_all x1, blocking collectives, local(): lax.all_to_all(by_target(values, piece_dest), DP, split_axis=0, concat_ax...  57.1 us
    psum x4, blocking collectives, over_axes(): value = lax.psum(value, axis)  40.2 us
    all_to_all x1, waiting for transfers between devices, local(): lax.all_to_all(by_target(rewards, piece_dest), DP, split_axis=0, concat_a...  39.4 us
    all_to_all x1, starting transfers between devices, local(): lax.all_to_all(by_target(per_row, piece_dest), DP, split_axis=0, concat_a...  12 us
    all_to_all x1, starting transfers between devices, local(): lax.all_to_all(by_target(rewards, piece_dest), DP, split_axis=0, concat_a...  8.16 us
    gather x3, local copies, waits for them, and re-layouts, by_target(): return jnp.take(pieces, source_slot, axis=0).reshape(array.shape)  6.2 us
    convert_element_type x1, other arithmetic, whiten(): white_advantage.astype(jnp.bfloat16)  5.93 us
    select_n x4, other arithmetic, by_target(): return jnp.take(pieces, source_slot, axis=0).reshape(array.shape)  5.38 us
  transfers between devices with their start and end apart: 2, of which 1 were waited for; matrix products, arithmetic and copies ran while one was open for 9% of the time, Pallas kernels for 0%

commit v1 on v0

v1 whole, which is shorter than its diff:
```python
import functools

import jax
import jax.numpy as jnp
from jax import lax
from jax.experimental import pallas as pl
from jax.experimental.pallas import tpu as pltpu
from jax.sharding import PartitionSpec as P

MESH = pl.DeviceIdType.MESH
HIGHEST = lax.Precision.HIGHEST
F32 = jnp.float32
BF16 = jnp.bfloat16
LANES = 128
NZ = 8


def dot(a, b, dims=(((1,), (0,)), ((), ())), precision=None):
    return lax.dot_general(a, b, dims, precision=precision, preferred_element_type=F32)


def iota(shape, dim):
    return lax.broadcasted_iota(jnp.int32, shape, dim)


def column(row):
    on = iota((LANES, LANES), 0) == iota((LANES, LANES), 1)
    return jnp.sum(jnp.where(on, row, 0.0), axis=1, keepdims=True)


def kernel(
    cfg, slots_ref, smalls_ref, r_hbm, v_hbm, out_r, out_a,
    rbuf, vbuf, send_r, send_a, vals, recv_r, recv_a,
    cols, scales, sums, chooser, member, stats, tsend, trecv, part, st_z, st_y, st_g,
    load_sem, bulk_send, bulk_recv, t_send, t_recv, g_send, g_recv, z_send, z_recv, y_send, y_recv,
):
    n_dp, n_group, piece, span, width = cfg
    rows = n_dp * piece
    n_y = n_dp // NZ
    me = lax.axis_index("dp")
    group = lax.axis_index("group")
    y, z = me // NZ, lax.rem(me, NZ)
    waves = 2 * span // width
    half = waves // 2

    def peer(k):
        return lax.rem(y + k // NZ, n_y) * NZ + lax.rem(z + lax.rem(k, NZ), NZ)

    load_r = pltpu.make_async_copy(r_hbm, rbuf, load_sem.at[0])
    load_v = pltpu.make_async_copy(v_hbm, vbuf, load_sem.at[1])
    load_r.start()
    load_v.start()

    barrier = pltpu.get_barrier_semaphore()

    def greet(k, c):
        pl.semaphore_signal(barrier, 1, device_id={"dp": peer(k)}, device_id_type=MESH)
        return c

    lax.fori_loop(1, n_dp, greet, 0)

    def greet_group(k, c):
        pl.semaphore_signal(
            barrier, 1, device_id={"group": lax.rem(group + k, n_group)}, device_id_type=MESH
        )
        return c

    lax.fori_loop(1, n_group, greet_group, 0)

    for b in range(2):
        for q in range(2):
            spread = jnp.broadcast_to(
                column(smalls_ref[2 * q + b : 2 * q + b + 1, :]), (LANES, LANES)
            )
            per = LANES // piece
            cols[q, per * b : per * (b + 1)] = spread.reshape(per, piece, LANES)

    load_r.wait()

    def gather_r(d, c):
        p = slots_ref[d]
        send_r[d] = rbuf[p]
        sums[0, d] = cols[0, p]
        sums[1, d] = cols[1, p]
        return c

    lax.fori_loop(0, n_dp, gather_r, 0)

    pl.semaphore_wait(barrier, n_dp - 1 + n_group - 1)

    def bulk(w, k):
        source, target = (send_r, recv_r) if w < half else (send_a, recv_a)
        lanes = pl.ds((w % half) * width, width)
        return pltpu.make_async_remote_copy(
            source.at[peer(k), :, lanes], target.at[me, :, lanes],
            bulk_send.at[w, k], bulk_recv.at[w, k],
            device_id={"dp": peer(k)}, device_id_type=MESH,
        )

    def start_wave(w):
        def go(k, c):
            bulk(w, k).start()
            return c

        lax.fori_loop(1, n_dp, go, 0)

    start_wave(0)

    load_v.wait()

    def gather_v(d, c):
        vals[d] = vbuf[slots_ref[d]]
        return c

    lax.fori_loop(0, n_dp, gather_v, 0)
    recv_r[me] = send_r[me]

    lane = iota((rows, LANES), 1)
    lane_f = lane.astype(F32)
    lengths = sums[0].reshape(rows, LANES).astype(jnp.int32)
    rate = sums[1].reshape(rows, LANES)
    cols[0] = sums[0]
    scales[0] = jnp.exp(-rate)
    scales[1] = jnp.exp(-rate * lane_f)
    scales[2] = jnp.exp(rate * lane_f)
    scales[3] = jnp.exp(-rate * (LANES - lane_f))
    sums[...] = jnp.zeros_like(sums)
    triangle = (iota((LANES, LANES), 0) >= iota((LANES, LANES), 1)).astype(F32)

    def block(i, carry):
        next_head, next_value = carry
        at = span // LANES - 1 - i
        lanes = pl.ds(pl.multiple_of(at * LANES, LANES), LANES)
        position = at * LANES + lane
        length = cols[0].reshape(rows, LANES).astype(jnp.int32)
        reward = send_r[:, :, lanes].astype(F32).reshape(rows, LANES)
        value = vals[:, :, lanes].astype(F32).reshape(rows, LANES)
        valid = position < length
        value_next = jnp.where(lane == LANES - 1, next_value, pltpu.roll(value, LANES - 1, 1))
        value_next = jnp.where(position + 1 < length, value_next, 0.0)
        td = jnp.where(valid, reward + scales[0] * value_next - value, 0.0)
        local = dot(td * scales[1], triangle, precision=HIGHEST) * scales[2]
        total = local + scales[3] * next_head
        rounded = jnp.where(valid, total, 0.0).astype(BF16)
        send_a[:, :, lanes] = rounded.reshape(n_dp, piece, LANES)
        reward = jnp.where(valid, reward, 0.0)
        kept = rounded.astype(F32)
        for q, term in enumerate((reward, kept, reward * reward, kept * kept)):
            sums[q] += term.reshape(n_dp, piece, LANES)
        return total[:, 0:1], value[:, 0:1]

    zero = jnp.zeros((rows, 1), F32)
    lax.fori_loop(0, span // LANES, block, (zero, zero))
    recv_a[me] = send_a[me]

    term_of, row_of = lane // piece, lax.rem(lane, piece)
    own = row_of == lax.rem(iota((rows, LANES), 0), piece)
    packed = jnp.where(own & (term_of == 0), cols[0].reshape(rows, LANES), 0.0)
    for q in range(4):
        total = jnp.sum(sums[q].reshape(rows, LANES), axis=1, keepdims=True)
        packed = jnp.where(own & (term_of == q + 1), total, packed)
    tsend[...] = jnp.sum(packed.reshape(n_dp, piece, LANES), axis=1, keepdims=True)

    for b in range(2):
        here = slice(b * LANES, (b + 1) * LANES)
        order = column(smalls_ref[6 + b : 7 + b, :]).astype(jnp.int32)
        chooser[b] = (order == iota((LANES, LANES), 1)).astype(BF16)
        batch = column(smalls_ref[4 + b : 5 + b, :]).astype(jnp.int32)
        member[here] = (batch == iota((LANES, LANES), 1)).astype(F32)

    def terms(k):
        return pltpu.make_async_remote_copy(
            tsend.at[peer(k)], trecv.at[me], t_send.at[k], t_recv.at[k],
            device_id={"dp": peer(k)}, device_id_type=MESH,
        )

    def terms_go(k, c):
        terms(k).start()
        return c

    def terms_wait(k, c):
        terms(k).wait()
        return c

    lax.fori_loop(1, n_dp, terms_go, 0)
    start_wave(1)
    trecv[me] = tsend[me]
    lax.fori_loop(1, n_dp, terms_wait, 0)

    spread = jnp.broadcast_to(trecv[...], (n_dp, piece, LANES)).reshape(rows, LANES)
    spread = jnp.where(own, spread, 0.0)
    select = (iota((LANES, LANES), 0) // piece == iota((LANES, LANES), 1)).astype(F32)
    totals = jnp.zeros((LANES, LANES), F32)
    for b in range(2):
        here = slice(b * LANES, (b + 1) * LANES)
        moved = dot(chooser[b].astype(F32), spread[here], precision=HIGHEST)
        moved = dot(moved, select, precision=HIGHEST)
        stats[4, here] = jnp.broadcast_to(moved[:, 0:1], (LANES, LANES))
        totals += dot(moved, member[here], (((0,), (0,)), ((), ())), precision=HIGHEST)

    def exchange(store, index, sizes, target, send_sem, recv_sem, between):
        store[index] = part[...]

        def copy(k):
            return pltpu.make_async_remote_copy(
                part, store.at[index], send_sem.at[k], recv_sem.at[k],
                device_id=target(k), device_id_type=MESH,
            )

        def go(k, c):
            copy(k).start()
            return c

        def done(k, c):
            copy(k).wait()
            return c

        lax.fori_loop(1, sizes, go, 0)
        between()
        lax.fori_loop(1, sizes, done, 0)
        part[...] = jnp.sum(store[...], axis=0)

    part[...] = totals[0:8]
    exchange(
        st_g, group, n_group, lambda k: {"group": lax.rem(group + k, n_group)},
        g_send, g_recv, lambda: None,
    )
    exchange(
        st_z, z, NZ, lambda k: {"dp": y * NZ + lax.rem(z + k, NZ)},
        z_send, z_recv, lambda: start_wave(2),
    )
    exchange(
        st_y, y, n_y, lambda k: {"dp": lax.rem(y + k, n_y) * NZ + z},
        y_send, y_recv, lambda: start_wave(3),
    )

    total = part[...]
    count = jnp.maximum(total[0:1], 1.0)
    for q in range(2):
        mean = total[1 + q : 2 + q] / count
        spread = total[3 + q : 4 + q] / count - mean * mean
        for s, value in enumerate((mean, lax.rsqrt(spread + 1e-05))):
            picked = jnp.sum(member[...] * value, axis=1, keepdims=True)
            stats[2 * q + s] = jnp.broadcast_to(picked, (rows, LANES))

    tile = 256
    for w in range(waves):
        def wait_wave(k, c):
            bulk(w, k).wait()
            return c

        lax.fori_loop(1, n_dp, wait_wave, 0)
        q = 0 if w < half else 1
        source, out = ((recv_r, out_r), (recv_a, out_a))[q]

        def finish(i, c):
            start = pl.multiple_of((w % half) * width + i * tile, LANES)
            for b in range(2):
                per = LANES // piece
                block = source[per * b : per * (b + 1), :, pl.ds(start, tile)]
                block = block.astype(F32).reshape(LANES, tile).astype(BF16)
                moved = dot(chooser[b], block)
                here = slice(b * LANES, (b + 1) * LANES)
                length = stats[4, here].astype(jnp.int32)
                for s in range(tile // LANES):
                    position = start + s * LANES + iota((LANES, LANES), 1)
                    white = (moved[:, s * LANES : (s + 1) * LANES] - stats[2 * q, here]) * stats[
                        2 * q + 1, here
                    ]
                    out[here, pl.ds(start + s * LANES, LANES)] = jnp.where(
                        position < length, white, 0.0
                    ).astype(BF16)
            return c

        lax.fori_loop(0, width // tile, finish, 0)


def local(rewards, values, lengths, decay_rate, piece_dest, row_perm, minibatch, *, n_dp, n_group):
    rows, span = rewards.shape
    piece = rows // n_dp
    width = span // 2
    slots = jnp.sum(
        jnp.where(
            piece_dest[0][None, :] == jnp.arange(n_dp, dtype=jnp.int32)[:, None],
            jnp.arange(n_dp, dtype=jnp.int32)[None, :],
            0,
        ),
        axis=1,
    )
    smalls = jnp.concatenate(
        [
            lengths.astype(F32).reshape(2, LANES),
            decay_rate.reshape(2, LANES),
            minibatch.astype(F32).reshape(2, LANES),
            row_perm.astype(F32),
        ],
        axis=0,
    )
    vmem = pl.BlockSpec(memory_space=pltpu.VMEM)
    hbm = pl.BlockSpec(memory_space=pl.ANY)
    bulk = pltpu.VMEM((n_dp, piece, span), BF16)
    dma = pltpu.SemaphoreType.DMA
    waves = 2 * span // width
    n_y = n_dp // NZ
    return pl.pallas_call(
        functools.partial(kernel, (n_dp, n_group, piece, span, width)),
        out_shape=(jax.ShapeDtypeStruct((rows, span), BF16),) * 2,
        in_specs=[pl.BlockSpec(memory_space=pltpu.SMEM), vmem, hbm, hbm],
        out_specs=(vmem, vmem),
        scratch_shapes=[bulk] * 7
        + [
            pltpu.VMEM((2, n_dp, piece, LANES), F32),
            pltpu.VMEM((4, rows, LANES), F32),
            pltpu.VMEM((4, n_dp, piece, LANES), F32),
            pltpu.VMEM((2, LANES, LANES), BF16),
            pltpu.VMEM((rows, LANES), F32),
            pltpu.VMEM((5, rows, LANES), F32),
            pltpu.VMEM((n_dp, 1, LANES), F32),
            pltpu.VMEM((n_dp, 1, LANES), F32),
            pltpu.VMEM((8, LANES), F32),
            pltpu.VMEM((NZ, 8, LANES), F32),
            pltpu.VMEM((n_y, 8, LANES), F32),
            pltpu.VMEM((n_group, 8, LANES), F32),
            dma((2,)),
            dma((waves, n_dp)), dma((waves, n_dp)),
            dma((n_dp,)), dma((n_dp,)),
            dma((n_group,)), dma((n_group,)),
            dma((NZ,)), dma((NZ,)),
            dma((n_y,)), dma((n_y,)),
        ],
        compiler_params=pltpu.CompilerParams(
            collective_id=0, has_side_effects=True, vmem_limit_bytes=40 * 2**20
        ),
        name="reshuffle",
    )(
        slots,
        smalls,
        rewards.reshape(n_dp, piece, span),
        values.reshape(n_dp, piece, span),
    )


def solution(mesh):
    both = ("dp", "group")
    return jax.shard_map(
        functools.partial(local, n_dp=mesh.shape["dp"], n_group=mesh.shape["group"]),
        mesh=mesh,
        in_specs=(
            P(both, None), P(both, None), P(both), P(both), P("dp", None), P(both, None), P(both),
        ),
        out_specs=(P(both, None), P(both, None)),
        check_vma=False,
    )
```

time: 211 us -> 118 us (0.56)
  Pallas kernels: 0 us -> 109 us
  blocking collectives: 97.3 us -> 0 us
  waiting for transfers between devices: 39.4 us -> 0 us
  starting transfers between devices: 20.2 us -> 0 us
  other arithmetic: 21.6 us -> 2.84 us
  local copies, waits for them, and re-layouts: 21 us -> 5.82 us
  matrix products: 8.92 us -> 0 us
    pallas_call x0 -> x1, Pallas kernels: none -> 109 us  [local(): pl.pallas_call(functools.partial(kernel, (n_dp, n_group, piece, span, wid...]
    all_to_all x1 -> x0, blocking collectives: 57.1 us -> none  [local(): lax.all_to_all(by_target(values, piece_dest), DP, split_axis=0, concat_ax...]
    psum x4 -> x0, blocking collectives: 40.2 us -> none  [over_axes(): value = lax.psum(value, axis)]
    all_to_all x2 -> x0, waiting for transfers between devices: 39.4 us -> none  [the longest x1 39.4 us: local(): lax.all_to_all(by_target(rewards, piece_dest), DP, split_axis=0, concat_a...]
    all_to_all x2 -> x0, starting transfers between devices: 20.2 us -> none  [the longest x1 12 us: local(): lax.all_to_all(by_target(per_row, piece_dest), DP, split_axis=0, concat_a...]
    dot_general x6 -> x0, matrix products: 8.92 us -> none  [the longest x2 5.36 us: permute_one(): jnp.einsum('bim,bmc->bic', chooser, shaped, preferred_element_type=jnp.fl...]
    select_n x7 -> x0, other arithmetic: 7.29 us -> none  [the longest x4 5.38 us: by_target(): return jnp.take(pieces, source_slot, axis=0).reshape(array.shape)]
    gather x4 -> x0, local copies, waits for them, and re-layouts: 6.92 us -> none  [the longest x3 6.2 us: by_target(): return jnp.take(pieces, source_slot, axis=0).reshape(array.shape)]
  transfers between devices with their start and end apart: 2 -> 0, of which waited for: 1 -> 0; matrix products, arithmetic and copies ran while one was open for 9% -> 0% of each run, Pallas kernels for 0% -> 0%
where the time goes in v1:
time: 118 us
  Pallas kernels  109 us (92%)
  local copies, waits for them, and re-layouts  5.82 us (5%)
  other arithmetic  2.84 us (2%)
    pallas_call x1, Pallas kernels, local(): pl.pallas_call(functools.partial(kernel, (n_dp, n_group, piece, span, wid...  109 us
    unnamed x6, local copies, waits for them, and re-layouts  5.82 us

profile of v1, /device:TPU:1, one launch (start us, length us, event | category | flops | bytes accessed | tf_op | source)
XLA Modules:
  0.0 118.0 jit_solution(12556909425154184727)
XLA Ops:
  0.6 0.8 select_reduce_fusion.slots_ref
  1.4 0.7 convert_element_type.11
  2.1 0.7 convert_bitcast_fusion
  2.8 0.7 pad_maximum_fusion.smalls_ref
  3.5 0.0 copy-start
  3.5 1.6 %copy-done = bf16[256,4096]{1,0:T(8,128)(2,1)S(1)} copy-done((bf16[256,4096]{1,0:T(8,128)(2,1)S(1)}, bf16[256,4096]{1,0:T(8,128)(2,1)}, u32[]{:S(2)}) %copy-start) | copy-done | bytes 2097176
  5.1 0.0 copy-start.1
  5.1 1.6 %copy-done.1 = bf16[256,4096]{1,0:T(8,128)(2,1)S(1)} copy-done((bf16[256,4096]{1,0:T(8,128)(2,1)S(1)}, bf16[256,4096]{1,0:T(8,128)(2,1)}, u32[]{:S(2)}) %copy-start.1) | copy-done | bytes 2097176
  6.7 108.7 %reshuffle.1 = (bf16[256,4096]{1,0:T(8,128)(2,1)S(1)}, bf16[256,4096]{1,0:T(8,128)(2,1)S(1)}) custom-call(s32[32]{0:T(128)S(1)} %select_reduce_fusion.slots_ref, f32[8,128]{1,0:T(8,128)S(1)} %pad_maximum_fusion.smalls_ref, bf16[32,8,4096]{2,1,0:T(8,128)(2,1)S(1)} %bitcast.8, bf16[32,8,4096]{2,1,0:T(8,128)(2,1)S(1)} %bitcast.9), custom_call_target="tpu_custom_call" | custom-call | tf_op jit(solution)/shard_map/reshuffle/pallas_call | solution.py:305
  115.3 1.3 %copy.11 = bf16[256,4096]{1,0:T(8,128)(2,1)} copy(bf16[256,4096]{1,0:T(8,128)(2,1)S(1)} %get-tuple-element.6) | data formatting | bytes 4194304
  116.6 1.3 %copy.12 = bf16[256,4096]{1,0:T(8,128)(2,1)} copy(bf16[256,4096]{1,0:T(8,128)(2,1)S(1)} %get-tuple-element.7) | data formatting | bytes 4194304
Async XLA Ops:
  3.5 1.6 %copy-start = (bf16[256,4096]{1,0:T(8,128)(2,1)S(1)}, bf16[256,4096]{1,0:T(8,128)(2,1)}, u32[]{:S(2)}) copy-start(bf16[256,4096]{1,0:T(8,128)(2,1)} %param.7) | copy-start | bytes 6291460
  5.1 1.6 %copy-start.1 = (bf16[256,4096]{1,0:T(8,128)(2,1)S(1)}, bf16[256,4096]{1,0:T(8,128)(2,1)}, u32[]{:S(2)}) copy-start(bf16[256,4096]{1,0:T(8,128)(2,1)} %param.8) | copy-start | bytes 6291460

commit v2 on v1

--- a/solution.py
+++ b/solution.py
@@ -29,8 +29,8 @@
 
 
 def kernel(
-    cfg, slots_ref, smalls_ref, r_hbm, v_hbm, out_r, out_a,
-    rbuf, vbuf, send_r, send_a, vals, recv_r, recv_a,
+    cfg, dest_hbm, len_hbm, rate_hbm, batch_hbm, perm_hbm, r_hbm, v_hbm, out_r, out_a,
+    dest_ref, slots_ref, len_ref, rate_ref, batch_ref, perm_ref, rbuf, vbuf, send_r, send_a, vals, recv_r, recv_a,
     cols, scales, sums, chooser, member, stats, tsend, trecv, part, st_z, st_y, st_g,
     load_sem, bulk_send, bulk_recv, t_send, t_recv, g_send, g_recv, z_send, z_recv, y_send, y_recv,
 ):
@@ -46,11 +46,6 @@
     def peer(k):
         return lax.rem(y + k // NZ, n_y) * NZ + lax.rem(z + lax.rem(k, NZ), NZ)
 
-    load_r = pltpu.make_async_copy(r_hbm, rbuf, load_sem.at[0])
-    load_v = pltpu.make_async_copy(v_hbm, vbuf, load_sem.at[1])
-    load_r.start()
-    load_v.start()
-
     barrier = pltpu.get_barrier_semaphore()
 
     def greet(k, c):
@@ -67,15 +62,47 @@
 
     lax.fori_loop(1, n_group, greet_group, 0)
 
+    pairs = (
+        (dest_hbm, dest_ref), (len_hbm, len_ref), (rate_hbm, rate_ref),
+        (batch_hbm, batch_ref), (perm_hbm, perm_ref),
+    )
+    smalls = [pltpu.make_async_copy(a, b, load_sem.at[i]) for i, (a, b) in enumerate(pairs)]
+    quarter = n_dp // 4
+
+    def load(q, i):
+        source, target = ((r_hbm, rbuf), (v_hbm, vbuf))[q]
+        pieces = pl.ds(i * quarter, quarter)
+        return pltpu.make_async_copy(
+            source.at[pieces], target.at[pieces], load_sem.at[5 + 4 * q + i]
+        )
+
+    for copy in smalls:
+        copy.start()
+    for i in range(4):
+        load(0, i).start()
+    for i in range(4):
+        load(1, i).start()
+
+    for copy in smalls:
+        copy.wait()
+
+    def invert(d, c):
+        slot = 0
+        for p in range(n_dp):
+            slot = jnp.where(dest_ref[0, p] == d, p, slot)
+        slots_ref[d] = slot
+        return c
+
+    lax.fori_loop(0, n_dp, invert, 0)
+
     for b in range(2):
-        for q in range(2):
-            spread = jnp.broadcast_to(
-                column(smalls_ref[2 * q + b : 2 * q + b + 1, :]), (LANES, LANES)
-            )
+        for q, ref in enumerate((len_ref, rate_ref)):
+            spread = jnp.broadcast_to(column(ref[b : b + 1, :].astype(F32)), (LANES, LANES))
             per = LANES // piece
             cols[q, per * b : per * (b + 1)] = spread.reshape(per, piece, LANES)
 
-    load_r.wait()
+    for i in range(4):
+        load(0, i).wait()
 
     def gather_r(d, c):
         p = slots_ref[d]
@@ -106,7 +133,8 @@
 
     start_wave(0)
 
-    load_v.wait()
+    for i in range(4):
+        load(1, i).wait()
 
     def gather_v(d, c):
         vals[d] = vbuf[slots_ref[d]]
@@ -163,9 +191,9 @@
 
     for b in range(2):
         here = slice(b * LANES, (b + 1) * LANES)
-        order = column(smalls_ref[6 + b : 7 + b, :]).astype(jnp.int32)
+        order = column(perm_ref[b : b + 1, :].astype(F32)).astype(jnp.int32)
         chooser[b] = (order == iota((LANES, LANES), 1)).astype(BF16)
-        batch = column(smalls_ref[4 + b : 5 + b, :]).astype(jnp.int32)
+        batch = column(batch_ref[b : b + 1, :].astype(F32)).astype(jnp.int32)
         member[here] = (batch == iota((LANES, LANES), 1)).astype(F32)
 
     def terms(k):
@@ -279,25 +307,8 @@
     rows, span = rewards.shape
     piece = rows // n_dp
     width = span // 2
-    slots = jnp.sum(
-        jnp.where(
-            piece_dest[0][None, :] == jnp.arange(n_dp, dtype=jnp.int32)[:, None],
-            jnp.arange(n_dp, dtype=jnp.int32)[None, :],
-            0,
-        ),
-        axis=1,
-    )
-    smalls = jnp.concatenate(
-        [
-            lengths.astype(F32).reshape(2, LANES),
-            decay_rate.reshape(2, LANES),
-            minibatch.astype(F32).reshape(2, LANES),
-            row_perm.astype(F32),
-        ],
-        axis=0,
-    )
     vmem = pl.BlockSpec(memory_space=pltpu.VMEM)
-    hbm = pl.BlockSpec(memory_space=pl.ANY)
+    hbm = pl.BlockSpec(memory_space=pltpu.HBM)
     bulk = pltpu.VMEM((n_dp, piece, span), BF16)
     dma = pltpu.SemaphoreType.DMA
     waves = 2 * span // width
@@ -305,9 +316,17 @@
     return pl.pallas_call(
         functools.partial(kernel, (n_dp, n_group, piece, span, width)),
         out_shape=(jax.ShapeDtypeStruct((rows, span), BF16),) * 2,
-        in_specs=[pl.BlockSpec(memory_space=pltpu.SMEM), vmem, hbm, hbm],
+        in_specs=[hbm] * 7,
         out_specs=(vmem, vmem),
-        scratch_shapes=[bulk] * 7
+        scratch_shapes=[
+            pltpu.SMEM((1, n_dp), jnp.int32),
+            pltpu.SMEM((n_dp,), jnp.int32),
+            pltpu.VMEM((2, LANES), jnp.int32),
+            pltpu.VMEM((2, LANES), F32),
+            pltpu.VMEM((2, LANES), jnp.int32),
+            pltpu.VMEM((2, LANES), jnp.int32),
+        ]
+        + [bulk] * 7
         + [
             pltpu.VMEM((2, n_dp, piece, LANES), F32),
             pltpu.VMEM((4, rows, LANES), F32),
@@ -321,7 +340,7 @@
             pltpu.VMEM((NZ, 8, LANES), F32),
             pltpu.VMEM((n_y, 8, LANES), F32),
             pltpu.VMEM((n_group, 8, LANES), F32),
-            dma((2,)),
+            dma((13,)),
             dma((waves, n_dp)), dma((waves, n_dp)),
             dma((n_dp,)), dma((n_dp,)),
             dma((n_group,)), dma((n_group,)),
@@ -333,10 +352,18 @@
         ),
         name="reshuffle",
     )(
-        slots,
-        smalls,
-        rewards.reshape(n_dp, piece, span),
-        values.reshape(n_dp, piece, span),
+        *(
+            pltpu.with_memory_space_constraint(array, pltpu.HBM)
+            for array in (
+                piece_dest,
+                lengths.reshape(2, LANES),
+                decay_rate.reshape(2, LANES),
+                minibatch.reshape(2, LANES),
+                row_perm,
+                rewards.reshape(n_dp, piece, span),
+                values.reshape(n_dp, piece, span),
+            )
+        )
     )
 
 

time: 118 us -> 111 us (0.941)
  local copies, waits for them, and re-layouts: 5.82 us -> 2.64 us
  other arithmetic: 2.84 us -> 0 us
    unnamed x6 -> x2, local copies, waits for them, and re-layouts: 5.82 us -> 2.64 us
where the time goes in v2:
time: 111 us
  Pallas kernels  108 us (97%)
  local copies, waits for them, and re-layouts  2.64 us (2%)
    pallas_call x1, Pallas kernels, local(): pl.pallas_call(functools.partial(kernel, (n_dp, n_group, piece, span, wid...  108 us
    unnamed x2, local copies, waits for them, and re-layouts  2.64 us

profile of v2, /device:TPU:1, one launch (start us, length us, event | category | flops | bytes accessed | tf_op | source)
XLA Modules:
  0.0 111.4 jit_solution(640481775893260305)
XLA Ops:
  0.6 108.1 %reshuffle.1 = (bf16[256,4096]{1,0:T(8,128)(2,1)S(1)}, bf16[256,4096]{1,0:T(8,128)(2,1)S(1)}) custom-call(s32[1,32]{1,0:T(1,128)} %dest_hbm.1, s32[2,128]{1,0:T(2,128)} %bitcast.7, f32[2,128]{1,0:T(2,128)} %bitcast.8, s32[2,128]{1,0:T(2,128)} %bitcast.9, s32[2,128]{1,0:T(2,128)} %perm_hbm.1, bf16[32,8,4096]{2,1,0:T(8,128)(2,1)} %bitcast.5, ...), custom_call_target="tpu_custom_call" | custom-call | tf_op jit(solution)/shard_map/reshuffle/pallas_call | solution.py:316
  108.7 1.3 %copy.11 = bf16[256,4096]{1,0:T(8,128)(2,1)} copy(bf16[256,4096]{1,0:T(8,128)(2,1)S(1)} %get-tuple-element.4) | data formatting | bytes 4194304
  110.0 1.3 %copy.12 = bf16[256,4096]{1,0:T(8,128)(2,1)} copy(bf16[256,4096]{1,0:T(8,128)(2,1)S(1)} %get-tuple-element.5) | data formatting | bytes 4194304

commit v3 on v2

--- a/solution.py
+++ b/solution.py
@@ -28,11 +28,23 @@
     return jnp.sum(jnp.where(on, row, 0.0), axis=1, keepdims=True)
 
 
+def whiten(block, chooser, mean, scale, length, start):
+    tile = block.shape[-1]
+    moved = dot(chooser, block.astype(F32).reshape(LANES, tile).astype(BF16))
+    done = []
+    for s in range(tile // LANES):
+        position = start + s * LANES + iota((LANES, LANES), 1)
+        white = (moved[:, s * LANES : (s + 1) * LANES] - mean) * scale
+        done.append(jnp.where(position < length, white, 0.0).astype(BF16))
+    return jnp.concatenate(done, axis=1)
+
+
 def kernel(
-    cfg, dest_hbm, len_hbm, rate_hbm, batch_hbm, perm_hbm, r_hbm, v_hbm, out_r, out_a,
+    cfg, dest_hbm, len_hbm, rate_hbm, batch_hbm, perm_hbm, r_hbm, v_hbm,
+    out_r, out_a, last, chooser, stats,
     dest_ref, slots_ref, len_ref, rate_ref, batch_ref, perm_ref, rbuf, vbuf, send_r, send_a, vals, recv_r, recv_a,
-    cols, scales, sums, chooser, member, stats, tsend, trecv, part, st_z, st_y, st_g,
-    load_sem, bulk_send, bulk_recv, t_send, t_recv, g_send, g_recv, z_send, z_recv, y_send, y_recv,
+    cols, scales, sums, member, stats_r, tsend, trecv, part, st_z, st_y, st_g,
+    load_sem, bulk_send, bulk_recv, t_send, t_recv, g_send, g_recv, z_send, z_recv, y_send, y_recv, ready,
 ):
     n_dp, n_group, piece, span, width = cfg
     rows = n_dp * piece
@@ -46,13 +58,33 @@
     def peer(k):
         return lax.rem(y + k // NZ, n_y) * NZ + lax.rem(z + lax.rem(k, NZ), NZ)
 
+    def near(k):
+        return lax.rem(k // 5 + n_y - 1, n_y) * NZ + lax.rem(lax.rem(k, 5) + NZ - 2, NZ)
+
+    def each_near(do):
+        def go(k, c):
+            do(near(k))
+            return c
+
+        lax.fori_loop(0, 7, go, 0)
+        lax.fori_loop(8, 15, go, 0)
+
+    def each_far(do):
+        def beside(k, c):
+            do(lax.rem(k // 3 + n_y - 1, n_y) * NZ + 3 + lax.rem(k, 3))
+            return c
+
+        def across(k, c):
+            do(2 * NZ + k)
+            return c
+
+        lax.fori_loop(0, 9, beside, 0)
+        lax.fori_loop(0, NZ, across, 0)
+
     barrier = pltpu.get_barrier_semaphore()
-
-    def greet(k, c):
-        pl.semaphore_signal(barrier, 1, device_id={"dp": peer(k)}, device_id_type=MESH)
-        return c
-
-    lax.fori_loop(1, n_dp, greet, 0)
+    each_near(
+        lambda k: pl.semaphore_signal(barrier, 1, device_id={"dp": peer(k)}, device_id_type=MESH)
+    )
 
     def greet_group(k, c):
         pl.semaphore_signal(
@@ -95,6 +127,48 @@
 
     lax.fori_loop(0, n_dp, invert, 0)
 
+    for i in range(4):
+        load(0, i).wait()
+
+    def gather_first(d, c):
+        send_r[d, :, 0:width] = rbuf[slots_ref[d], :, 0:width]
+        return c
+
+    lax.fori_loop(0, n_dp, gather_first, 0)
+
+    pl.semaphore_wait(barrier, 14 + n_group - 1)
+    each_near(
+        lambda k: pl.semaphore_signal(ready, 1, device_id={"dp": peer(k)}, device_id_type=MESH)
+    )
+
+    def bulk(w, k):
+        source, target = (send_r, recv_r) if w < half else (send_a, recv_a)
+        lanes = pl.ds((w % half) * width, width)
+        landing = last.at[me] if w == waves - 1 else target.at[me, :, lanes]
+        return pltpu.make_async_remote_copy(
+            source.at[peer(k), :, lanes], landing,
+            bulk_send.at[w, k], bulk_recv.at[w, k],
+            device_id={"dp": peer(k)}, device_id_type=MESH,
+        )
+
+    def start_wave(w):
+        def go(k, c):
+            bulk(w, k).start()
+            return c
+
+        lax.fori_loop(1, n_dp, go, 0)
+
+    each_near(lambda k: bulk(0, k).start())
+
+    def gather_rest(d, c):
+        send_r[d, :, width:span] = rbuf[slots_ref[d], :, width:span]
+        return c
+
+    lax.fori_loop(0, n_dp, gather_rest, 0)
+
+    pl.semaphore_wait(ready, 14)
+    each_far(lambda k: bulk(0, k).start())
+
     for b in range(2):
         for q, ref in enumerate((len_ref, rate_ref)):
             spread = jnp.broadcast_to(column(ref[b : b + 1, :].astype(F32)), (LANES, LANES))
@@ -102,42 +176,13 @@
             cols[q, per * b : per * (b + 1)] = spread.reshape(per, piece, LANES)
 
     for i in range(4):
-        load(0, i).wait()
-
-    def gather_r(d, c):
+        load(1, i).wait()
+
+    def gather_v(d, c):
         p = slots_ref[d]
-        send_r[d] = rbuf[p]
+        vals[d] = vbuf[p]
         sums[0, d] = cols[0, p]
         sums[1, d] = cols[1, p]
-        return c
-
-    lax.fori_loop(0, n_dp, gather_r, 0)
-
-    pl.semaphore_wait(barrier, n_dp - 1 + n_group - 1)
-
-    def bulk(w, k):
-        source, target = (send_r, recv_r) if w < half else (send_a, recv_a)
-        lanes = pl.ds((w % half) * width, width)
-        return pltpu.make_async_remote_copy(
-            source.at[peer(k), :, lanes], target.at[me, :, lanes],
-            bulk_send.at[w, k], bulk_recv.at[w, k],
-            device_id={"dp": peer(k)}, device_id_type=MESH,
-        )
-
-    def start_wave(w):
-        def go(k, c):
-            bulk(w, k).start()
-            return c
-
-        lax.fori_loop(1, n_dp, go, 0)
-
-    start_wave(0)
-
-    for i in range(4):
-        load(1, i).wait()
-
-    def gather_v(d, c):
-        vals[d] = vbuf[slots_ref[d]]
         return c
 
     lax.fori_loop(0, n_dp, gather_v, 0)
@@ -179,7 +224,8 @@
 
     zero = jnp.zeros((rows, 1), F32)
     lax.fori_loop(0, span // LANES, block, (zero, zero))
-    recv_a[me] = send_a[me]
+    recv_a[me] = send_a[me, :, 0 : span - width]
+    last[me] = send_a[me, :, span - width : span]
 
     term_of, row_of = lane // piece, lax.rem(lane, piece)
     own = row_of == lax.rem(iota((rows, LANES), 0), piece)
@@ -223,7 +269,7 @@
         here = slice(b * LANES, (b + 1) * LANES)
         moved = dot(chooser[b].astype(F32), spread[here], precision=HIGHEST)
         moved = dot(moved, select, precision=HIGHEST)
-        stats[4, here] = jnp.broadcast_to(moved[:, 0:1], (LANES, LANES))
+        stats[2, here] = jnp.broadcast_to(moved[:, 0:1], (LANES, LANES))
         totals += dot(moved, member[here], (((0,), (0,)), ((), ())), precision=HIGHEST)
 
     def exchange(store, index, sizes, target, send_sem, recv_sem, between):
@@ -269,7 +315,7 @@
         spread = total[3 + q : 4 + q] / count - mean * mean
         for s, value in enumerate((mean, lax.rsqrt(spread + 1e-05))):
             picked = jnp.sum(member[...] * value, axis=1, keepdims=True)
-            stats[2 * q + s] = jnp.broadcast_to(picked, (rows, LANES))
+            (stats_r, stats)[q][s] = jnp.broadcast_to(picked, (rows, LANES))
 
     tile = 256
     for w in range(waves):
@@ -278,29 +324,52 @@
             return c
 
         lax.fori_loop(1, n_dp, wait_wave, 0)
-        q = 0 if w < half else 1
-        source, out = ((recv_r, out_r), (recv_a, out_a))[q]
+        if w == waves - 1:
+            break
+        source, out, moments = ((recv_r, out_r, stats_r), (recv_a, out_a, stats))[w // half]
 
         def finish(i, c):
             start = pl.multiple_of((w % half) * width + i * tile, LANES)
             for b in range(2):
                 per = LANES // piece
-                block = source[per * b : per * (b + 1), :, pl.ds(start, tile)]
-                block = block.astype(F32).reshape(LANES, tile).astype(BF16)
-                moved = dot(chooser[b], block)
                 here = slice(b * LANES, (b + 1) * LANES)
-                length = stats[4, here].astype(jnp.int32)
-                for s in range(tile // LANES):
-                    position = start + s * LANES + iota((LANES, LANES), 1)
-                    white = (moved[:, s * LANES : (s + 1) * LANES] - stats[2 * q, here]) * stats[
-                        2 * q + 1, here
-                    ]
-                    out[here, pl.ds(start + s * LANES, LANES)] = jnp.where(
-                        position < length, white, 0.0
-                    ).astype(BF16)
+                out[here, pl.ds(start, tile)] = whiten(
+                    source[per * b : per * (b + 1), :, pl.ds(start, tile)], chooser[b],
+                    moments[0, here], moments[1, here], stats[2, here].astype(jnp.int32), start,
+                )
             return c
 
         lax.fori_loop(0, width // tile, finish, 0)
+
+
+def finish_kernel(cfg, white_r, white_a, last, chooser, stats, out_r, out_a, white, sem):
+    piece, span, width = cfg
+    rows = white_r.shape[0]
+    ready = span - width
+    copies = []
+
+    def send(source, target):
+        copy = pltpu.make_async_copy(source, target, sem.at[len(copies)])
+        copy.start()
+        copies.append(copy)
+
+    for i in range(4):
+        here = pl.ds(i * (rows // 4), rows // 4)
+        send(white_r.at[here], out_r.at[here])
+        send(white_a.at[here], out_a.at[here, 0:ready])
+    tile = 512
+    for i in range(width // tile):
+        lanes = slice(i * tile, (i + 1) * tile)
+        for b in range(2):
+            per = LANES // piece
+            here = slice(b * LANES, (b + 1) * LANES)
+            white[here, lanes] = whiten(
+                last[per * b : per * (b + 1), :, lanes], chooser[b],
+                stats[0, here], stats[1, here], stats[2, here].astype(jnp.int32), ready + i * tile,
+            )
+        send(white.at[:, lanes], out_a.at[:, ready + i * tile : ready + (i + 1) * tile])
+    for copy in copies:
+        copy.wait()
 
 
 def local(rewards, values, lengths, decay_rate, piece_dest, row_perm, minibatch, *, n_dp, n_group):
@@ -313,11 +382,18 @@
     dma = pltpu.SemaphoreType.DMA
     waves = 2 * span // width
     n_y = n_dp // NZ
-    return pl.pallas_call(
+    result = jax.ShapeDtypeStruct((rows, span), BF16)
+    parts = pl.pallas_call(
         functools.partial(kernel, (n_dp, n_group, piece, span, width)),
-        out_shape=(jax.ShapeDtypeStruct((rows, span), BF16),) * 2,
+        out_shape=(
+            result,
+            jax.ShapeDtypeStruct((rows, span - width), BF16),
+            jax.ShapeDtypeStruct((n_dp, piece, width), BF16),
+            jax.ShapeDtypeStruct((2, LANES, LANES), BF16),
+            jax.ShapeDtypeStruct((3, rows, LANES), F32),
+        ),
         in_specs=[hbm] * 7,
-        out_specs=(vmem, vmem),
+        out_specs=(vmem,) * 5,
         scratch_shapes=[
             pltpu.SMEM((1, n_dp), jnp.int32),
             pltpu.SMEM((n_dp,), jnp.int32),
@@ -326,14 +402,14 @@
             pltpu.VMEM((2, LANES), jnp.int32),
             pltpu.VMEM((2, LANES), jnp.int32),
         ]
-        + [bulk] * 7
+        + [bulk] * 6
         + [
+            pltpu.VMEM((n_dp, piece, span - width), BF16),
             pltpu.VMEM((2, n_dp, piece, LANES), F32),
             pltpu.VMEM((4, rows, LANES), F32),
             pltpu.VMEM((4, n_dp, piece, LANES), F32),
-            pltpu.VMEM((2, LANES, LANES), BF16),
             pltpu.VMEM((rows, LANES), F32),
-            pltpu.VMEM((5, rows, LANES), F32),
+            pltpu.VMEM((2, rows, LANES), F32),
             pltpu.VMEM((n_dp, 1, LANES), F32),
             pltpu.VMEM((n_dp, 1, LANES), F32),
             pltpu.VMEM((8, LANES), F32),
@@ -346,6 +422,7 @@
             dma((n_group,)), dma((n_group,)),
             dma((NZ,)), dma((NZ,)),
             dma((n_y,)), dma((n_y,)),
+            pltpu.SemaphoreType.REGULAR,
         ],
         compiler_params=pltpu.CompilerParams(
             collective_id=0, has_side_effects=True, vmem_limit_bytes=40 * 2**20
@@ -365,6 +442,15 @@
             )
         )
     )
+    return pl.pallas_call(
+        functools.partial(finish_kernel, (piece, span, width)),
+        out_shape=(result, result),
+        in_specs=[vmem] * 5,
+        out_specs=(hbm, hbm),
+        scratch_shapes=[pltpu.VMEM((rows, width), BF16), dma((12,))],
+        compiler_params=pltpu.CompilerParams(vmem_limit_bytes=16 * 2**20),
+        name="finish",
+    )(*parts)
 
 
 def solution(mesh):

time: 111 us -> 110 us (level)
  local copies, waits for them, and re-layouts: 2.64 us -> 0 us
    unnamed x2 -> x0, local copies, waits for them, and re-layouts: 2.64 us -> none
    pallas_call x0 -> x1, Pallas kernels: none -> 2.1 us  [local(): pl.pallas_call(functools.partial(finish_kernel, (piece, span, width)), ou...]
    pallas_call x1, Pallas kernels: 108 us -> 107 us  [local(): pl.pallas_call(functools.partial(kernel, (n_dp, n_group, piece, span, wid...]
where the time goes in v3:
time: 110 us
  Pallas kernels  109 us (99%)
    pallas_call x1, Pallas kernels, local(): pl.pallas_call(functools.partial(kernel, (n_dp, n_group, piece, span, wid...  107 us

profile of v3, /device:TPU:1, one launch (start us, length us, event | category | flops | bytes accessed | tf_op | source)
XLA Modules:
  0.0 109.7 jit_solution(11591581157696482361)
XLA Ops:
  0.6 106.9 %reshuffle.1 = (bf16[256,4096]{1,0:T(8,128)(2,1)S(1)}, bf16[256,2048]{1,0:T(8,128)(2,1)S(1)}, bf16[32,8,2048]{2,1,0:T(8,128)(2,1)S(1)}, bf16[2,128,128]{2,1,0:T(8,128)(2,1)S(1)}, f32[3,256,128]{2,1,0:T(8,128)S(1)}) custom-call(s32[1,32]{1,0:T(1,128)} %dest_hbm.1, s32[2,128]{1,0:T(2,128)} %bitcast.7, f32[2,128]{1,0:T(2,128)} %bitcast.8, s32[2,128]{1,0:T(2,128)} %bitcast.9, ...), custom_call_target="tpu_custom_call" | custom-call | tf_op jit(solution)/shard_map/reshuffle/pallas_call | solution.py:386
  107.6 2.1 %finish.1 = (bf16[256,4096]{1,0:T(8,128)(2,1)}, bf16[256,4096]{1,0:T(8,128)(2,1)}) custom-call(bf16[256,4096]{1,0:T(8,128)(2,1)S(1)} %get-tuple-element.7.white_r, bf16[256,2048]{1,0:T(8,128)(2,1)S(1)} %get-tuple-element.8.white_a, bf16[32,8,2048]{2,1,0:T(8,128)(2,1)S(1)} %get-tuple-element.9.last, bf16[2,128,128]{2,1,0:T(8,128)(2,1)S(1)} %get-tuple-element.10.chooser, ...), custom_call_target="tpu_custom_call" | custom-call | tf_op jit(solution)/shard_map/finish/pallas_call | solution.py:445

commit v4 on v3

--- a/solution.py
+++ b/solution.py
@@ -13,6 +13,9 @@
 BF16 = jnp.bfloat16
 LANES = 128
 NZ = 8
+CHUNKS = ((0, 0, 1), (0, 1, 1), (0, 2, 2), (1, 0, 2), (1, 2, 2))
+STRAIGHT = ((0, 0, 4), (1, 0, 2), (1, 2, 2))
+STEPS = (4, 3, 5, 2, 6, 1, 7)
 
 
 def dot(a, b, dims=(((1,), (0,)), ((), ())), precision=None):
@@ -28,9 +31,13 @@
     return jnp.sum(jnp.where(on, row, 0.0), axis=1, keepdims=True)
 
 
-def whiten(block, chooser, mean, scale, length, start):
+def whiten(source, y, b, lanes, chooser, mean, scale, length, start):
+    n_y = source.shape[0]
+    half = n_y // 2
+    pieces = [source[lax.rem(y - b * half - h + n_y, n_y), :, :, lanes] for h in range(half)]
+    block = jnp.concatenate([p.astype(F32) for p in pieces], axis=0)
     tile = block.shape[-1]
-    moved = dot(chooser, block.astype(F32).reshape(LANES, tile).astype(BF16))
+    moved = dot(chooser, block.reshape(LANES, tile).astype(BF16))
     done = []
     for s in range(tile // LANES):
         position = start + s * LANES + iota((LANES, LANES), 1)
@@ -43,48 +50,41 @@
     cfg, dest_hbm, len_hbm, rate_hbm, batch_hbm, perm_hbm, r_hbm, v_hbm,
     out_r, out_a, last, chooser, stats,
     dest_ref, slots_ref, len_ref, rate_ref, batch_ref, perm_ref, rbuf, vbuf, send_r, send_a, vals, recv_r, recv_a,
-    cols, scales, sums, member, stats_r, tsend, trecv, part, st_z, st_y, st_g,
-    load_sem, bulk_send, bulk_recv, t_send, t_recv, g_send, g_recv, z_send, z_recv, y_send, y_recv, ready,
+    relay_0, relay_1, relay_2, relay_3, relay_4,
+    cols, scales, sums, member, stats_r, tsend, trelay, trecv, part, st_z, st_y, st_g,
+    load_sem, y_leg_send, y_leg_recv, z_leg_send, z_leg_recv, a_send, a_recv,
+    t1_send, t1_recv, t2_send, t2_recv, g_send, g_recv, z_send, z_recv, y_send, y_recv,
 ):
-    n_dp, n_group, piece, span, width = cfg
+    n_dp, n_group, piece, span = cfg
     rows = n_dp * piece
     n_y = n_dp // NZ
+    unit = span // 4
+    relays = (relay_0, relay_1, relay_2, relay_3, relay_4)
+    final = len(CHUNKS) - 1
     me = lax.axis_index("dp")
     group = lax.axis_index("group")
     y, z = me // NZ, lax.rem(me, NZ)
-    waves = 2 * span // width
-    half = waves // 2
-
-    def peer(k):
-        return lax.rem(y + k // NZ, n_y) * NZ + lax.rem(z + lax.rem(k, NZ), NZ)
-
-    def near(k):
-        return lax.rem(k // 5 + n_y - 1, n_y) * NZ + lax.rem(lax.rem(k, 5) + NZ - 2, NZ)
-
-    def each_near(do):
-        def go(k, c):
-            do(near(k))
-            return c
-
-        lax.fori_loop(0, 7, go, 0)
-        lax.fori_loop(8, 15, go, 0)
-
-    def each_far(do):
-        def beside(k, c):
-            do(lax.rem(k // 3 + n_y - 1, n_y) * NZ + 3 + lax.rem(k, 3))
-            return c
-
-        def across(k, c):
-            do(2 * NZ + k)
-            return c
-
-        lax.fori_loop(0, 9, beside, 0)
-        lax.fori_loop(0, NZ, across, 0)
+
+    def along_y(j):
+        return lax.rem(y + j, n_y)
+
+    def along_z(k):
+        return lax.rem(z + k, NZ)
+
+    def remote(source, target, send_sem, recv_sem, place):
+        return pltpu.make_async_remote_copy(
+            source, target, send_sem, recv_sem, device_id=place, device_id_type=MESH
+        )
 
     barrier = pltpu.get_barrier_semaphore()
-    each_near(
-        lambda k: pl.semaphore_signal(barrier, 1, device_id={"dp": peer(k)}, device_id_type=MESH)
-    )
+    for j in range(1, n_y):
+        pl.semaphore_signal(
+            barrier, 1, device_id={"dp": along_y(j) * NZ + z}, device_id_type=MESH
+        )
+    for k in range(1, NZ):
+        pl.semaphore_signal(
+            barrier, 1, device_id={"dp": y * NZ + along_z(k)}, device_id_type=MESH
+        )
 
     def greet_group(k, c):
         pl.semaphore_signal(
@@ -130,44 +130,64 @@
     for i in range(4):
         load(0, i).wait()
 
-    def gather_first(d, c):
-        send_r[d, :, 0:width] = rbuf[slots_ref[d], :, 0:width]
+    def gather_r(d, c):
+        send_r[d] = rbuf[slots_ref[d]]
         return c
 
-    lax.fori_loop(0, n_dp, gather_first, 0)
-
-    pl.semaphore_wait(barrier, 14 + n_group - 1)
-    each_near(
-        lambda k: pl.semaphore_signal(ready, 1, device_id={"dp": peer(k)}, device_id_type=MESH)
-    )
-
-    def bulk(w, k):
-        source, target = (send_r, recv_r) if w < half else (send_a, recv_a)
-        lanes = pl.ds((w % half) * width, width)
-        landing = last.at[me] if w == waves - 1 else target.at[me, :, lanes]
-        return pltpu.make_async_remote_copy(
-            source.at[peer(k), :, lanes], landing,
-            bulk_send.at[w, k], bulk_recv.at[w, k],
-            device_id={"dp": peer(k)}, device_id_type=MESH,
-        )
-
-    def start_wave(w):
-        def go(k, c):
-            bulk(w, k).start()
-            return c
-
-        lax.fori_loop(1, n_dp, go, 0)
-
-    each_near(lambda k: bulk(0, k).start())
-
-    def gather_rest(d, c):
-        send_r[d, :, width:span] = rbuf[slots_ref[d], :, width:span]
-        return c
-
-    lax.fori_loop(0, n_dp, gather_rest, 0)
-
-    pl.semaphore_wait(ready, 14)
-    each_far(lambda k: bulk(0, k).start())
+    lax.fori_loop(0, n_dp, gather_r, 0)
+
+    pl.semaphore_wait(barrier, n_y - 1 + NZ - 1 + n_group - 1)
+
+    def y_leg(w, j):
+        q, first, width = CHUNKS[w]
+        source = (send_r, send_a)[q].at[pl.ds(along_y(j) * NZ, NZ), :, pl.ds(first * unit, width * unit)]
+        return remote(
+            source, relays[w].at[j - 1], y_leg_send.at[w, j], y_leg_recv.at[w, j],
+            {"dp": along_y(j) * NZ + z},
+        )
+
+    def z_leg(w, k):
+        q, first, width = CHUNKS[w]
+        lanes = pl.ds(first * unit, width * unit)
+        others = pl.ds(1, n_y - 1)
+        target = last.at[others, z] if w == final else (recv_r, recv_a)[q].at[others, z, :, lanes]
+        return remote(
+            relays[w].at[:, along_z(k)], target, z_leg_send.at[w, k], z_leg_recv.at[w, k],
+            {"dp": y * NZ + along_z(k)},
+        )
+
+    def straight(p, k):
+        q, first, width = STRAIGHT[p]
+        source = (send_r, send_a)[q].at[y * NZ + along_z(k), :, pl.ds(first * unit, width * unit)]
+        return remote(
+            source, (recv_r, recv_a, last)[p].at[0, z], a_send.at[p, k], a_recv.at[p, k],
+            {"dp": y * NZ + along_z(k)},
+        )
+
+    def start_y_leg(w):
+        for j in range(1, n_y):
+            y_leg(w, j).start()
+
+    def start_straight(p):
+        for k in STEPS:
+            straight(p, k).start()
+
+    def forward(w):
+        for j in range(1, n_y):
+            y_leg(w, j).wait_recv()
+        for k in STEPS:
+            z_leg(w, k).start()
+        q, first, width = CHUNKS[w]
+        for j in range(1, n_y):
+            if w == final:
+                last[j, z] = relays[w][j - 1, z]
+            else:
+                (recv_r, recv_a)[q][j, z, :, first * unit : (first + width) * unit] = relays[w][j - 1, z]
+
+    start_y_leg(0)
+    start_straight(0)
+    start_y_leg(1)
+    start_y_leg(2)
 
     for b in range(2):
         for q, ref in enumerate((len_ref, rate_ref)):
@@ -186,7 +206,7 @@
         return c
 
     lax.fori_loop(0, n_dp, gather_v, 0)
-    recv_r[me] = send_r[me]
+    recv_r[0, z] = send_r[me]
 
     lane = iota((rows, LANES), 1)
     lane_f = lane.astype(F32)
@@ -223,9 +243,14 @@
         return total[:, 0:1], value[:, 0:1]
 
     zero = jnp.zeros((rows, 1), F32)
-    lax.fori_loop(0, span // LANES, block, (zero, zero))
-    recv_a[me] = send_a[me, :, 0 : span - width]
-    last[me] = send_a[me, :, span - width : span]
+    third = span // LANES // 3
+    carry = lax.fori_loop(0, third, block, (zero, zero))
+    forward(0)
+    carry = lax.fori_loop(third, 2 * third, block, carry)
+    forward(1)
+    lax.fori_loop(2 * third, span // LANES, block, carry)
+    recv_a[0, z] = send_a[me, :, 0 : span // 2]
+    last[0, z] = send_a[me, :, span // 2 : span]
 
     term_of, row_of = lane // piece, lax.rem(lane, piece)
     own = row_of == lax.rem(iota((rows, LANES), 0), piece)
@@ -242,26 +267,35 @@
         batch = column(batch_ref[b : b + 1, :].astype(F32)).astype(jnp.int32)
         member[here] = (batch == iota((LANES, LANES), 1)).astype(F32)
 
-    def terms(k):
-        return pltpu.make_async_remote_copy(
-            tsend.at[peer(k)], trecv.at[me], t_send.at[k], t_recv.at[k],
-            device_id={"dp": peer(k)}, device_id_type=MESH,
-        )
-
-    def terms_go(k, c):
-        terms(k).start()
-        return c
-
-    def terms_wait(k, c):
-        terms(k).wait()
-        return c
-
-    lax.fori_loop(1, n_dp, terms_go, 0)
-    start_wave(1)
-    trecv[me] = tsend[me]
-    lax.fori_loop(1, n_dp, terms_wait, 0)
-
-    spread = jnp.broadcast_to(trecv[...], (n_dp, piece, LANES)).reshape(rows, LANES)
+    def terms_y(j):
+        return remote(
+            tsend.at[pl.ds(along_y(j) * NZ, NZ)], trelay.at[j], t1_send.at[j], t1_recv.at[j],
+            {"dp": along_y(j) * NZ + z},
+        )
+
+    def terms_z(k):
+        return remote(
+            trelay.at[:, along_z(k)], trecv.at[:, z], t2_send.at[k], t2_recv.at[k],
+            {"dp": y * NZ + along_z(k)},
+        )
+
+    trelay[0] = tsend[pl.ds(y * NZ, NZ)]
+    for j in range(1, n_y):
+        terms_y(j).start()
+    start_y_leg(3)
+    start_y_leg(4)
+    for j in range(1, n_y):
+        terms_y(j).wait()
+    for k in STEPS:
+        terms_z(k).start()
+    forward(2)
+    trecv[:, z] = trelay[:, z]
+    for k in STEPS:
+        terms_z(k).wait()
+
+    ordered = [trecv[lax.rem(y - h + n_y, n_y)] for h in range(n_y)]
+    spread = jnp.concatenate(ordered, axis=0)
+    spread = jnp.broadcast_to(spread, (n_dp, piece, LANES)).reshape(rows, LANES)
     spread = jnp.where(own, spread, 0.0)
     select = (iota((LANES, LANES), 0) // piece == iota((LANES, LANES), 1)).astype(F32)
     totals = jnp.zeros((LANES, LANES), F32)
@@ -299,14 +333,17 @@
         st_g, group, n_group, lambda k: {"group": lax.rem(group + k, n_group)},
         g_send, g_recv, lambda: None,
     )
+    def advantage_straight():
+        start_straight(1)
+        start_straight(2)
+
     exchange(
-        st_z, z, NZ, lambda k: {"dp": y * NZ + lax.rem(z + k, NZ)},
-        z_send, z_recv, lambda: start_wave(2),
+        st_z, z, NZ, lambda k: {"dp": y * NZ + along_z(k)}, z_send, z_recv, advantage_straight
     )
     exchange(
-        st_y, y, n_y, lambda k: {"dp": lax.rem(y + k, n_y) * NZ + z},
-        y_send, y_recv, lambda: start_wave(3),
+        st_y, y, n_y, lambda k: {"dp": along_y(k) * NZ + z}, y_send, y_recv, lambda: forward(3)
     )
+    forward(final)
 
     total = part[...]
     count = jnp.maximum(total[0:1], 1.0)
@@ -318,34 +355,37 @@
             (stats_r, stats)[q][s] = jnp.broadcast_to(picked, (rows, LANES))
 
     tile = 256
-    for w in range(waves):
-        def wait_wave(k, c):
-            bulk(w, k).wait()
-            return c
-
-        lax.fori_loop(1, n_dp, wait_wave, 0)
-        if w == waves - 1:
+    for w, (q, first, width) in enumerate(CHUNKS):
+        for p, (kind, begin, _) in enumerate(STRAIGHT):
+            if (kind, begin) == (q, first):
+                for k in STEPS:
+                    straight(p, k).wait()
+        for k in STEPS:
+            z_leg(w, k).wait()
+        if w == final:
             break
-        source, out, moments = ((recv_r, out_r, stats_r), (recv_a, out_a, stats))[w // half]
+        source, out, moments = ((recv_r, out_r, stats_r), (recv_a, out_a, stats))[q]
 
         def finish(i, c):
-            start = pl.multiple_of((w % half) * width + i * tile, LANES)
+            start = pl.multiple_of(first * unit + i * tile, LANES)
             for b in range(2):
-                per = LANES // piece
                 here = slice(b * LANES, (b + 1) * LANES)
                 out[here, pl.ds(start, tile)] = whiten(
-                    source[per * b : per * (b + 1), :, pl.ds(start, tile)], chooser[b],
+                    source, y, b, pl.ds(start, tile), chooser[b],
                     moments[0, here], moments[1, here], stats[2, here].astype(jnp.int32), start,
                 )
             return c
 
-        lax.fori_loop(0, width // tile, finish, 0)
-
-
-def finish_kernel(cfg, white_r, white_a, last, chooser, stats, out_r, out_a, white, sem):
-    piece, span, width = cfg
-    rows = white_r.shape[0]
-    ready = span - width
+        lax.fori_loop(0, width * unit // tile, finish, 0)
+    for w in range(len(CHUNKS)):
+        for j in range(1, n_y):
+            y_leg(w, j).wait_send()
+
+
+def finish_kernel(n_dp, white_r, white_a, last, chooser, stats, out_r, out_a, white, sem):
+    rows, width = white.shape
+    ready = white_a.shape[1]
+    y = lax.axis_index("dp") // NZ
     copies = []
 
     def send(source, target):
@@ -361,10 +401,9 @@
     for i in range(width // tile):
         lanes = slice(i * tile, (i + 1) * tile)
         for b in range(2):
-            per = LANES // piece
             here = slice(b * LANES, (b + 1) * LANES)
             white[here, lanes] = whiten(
-                last[per * b : per * (b + 1), :, lanes], chooser[b],
+                last, y, b, lanes, chooser[b],
                 stats[0, here], stats[1, here], stats[2, here].astype(jnp.int32), ready + i * tile,
             )
         send(white.at[:, lanes], out_a.at[:, ready + i * tile : ready + (i + 1) * tile])
@@ -375,20 +414,21 @@
 def local(rewards, values, lengths, decay_rate, piece_dest, row_perm, minibatch, *, n_dp, n_group):
     rows, span = rewards.shape
     piece = rows // n_dp
-    width = span // 2
+    half = span // 2
+    unit = span // 4
+    n_y = n_dp // NZ
     vmem = pl.BlockSpec(memory_space=pltpu.VMEM)
     hbm = pl.BlockSpec(memory_space=pltpu.HBM)
     bulk = pltpu.VMEM((n_dp, piece, span), BF16)
     dma = pltpu.SemaphoreType.DMA
-    waves = 2 * span // width
-    n_y = n_dp // NZ
+    chunks = len(CHUNKS)
     result = jax.ShapeDtypeStruct((rows, span), BF16)
     parts = pl.pallas_call(
-        functools.partial(kernel, (n_dp, n_group, piece, span, width)),
+        functools.partial(kernel, (n_dp, n_group, piece, span)),
         out_shape=(
             result,
-            jax.ShapeDtypeStruct((rows, span - width), BF16),
-            jax.ShapeDtypeStruct((n_dp, piece, width), BF16),
+            jax.ShapeDtypeStruct((rows, half), BF16),
+            jax.ShapeDtypeStruct((n_y, NZ, piece, half), BF16),
             jax.ShapeDtypeStruct((2, LANES, LANES), BF16),
             jax.ShapeDtypeStruct((3, rows, LANES), F32),
         ),
@@ -402,27 +442,34 @@
             pltpu.VMEM((2, LANES), jnp.int32),
             pltpu.VMEM((2, LANES), jnp.int32),
         ]
-        + [bulk] * 6
+        + [bulk] * 5
         + [
-            pltpu.VMEM((n_dp, piece, span - width), BF16),
+            pltpu.VMEM((n_y, NZ, piece, span), BF16),
+            pltpu.VMEM((n_y, NZ, piece, half), BF16),
+        ]
+        + [pltpu.VMEM((n_y - 1, NZ, piece, w * unit), BF16) for _, _, w in CHUNKS]
+        + [
             pltpu.VMEM((2, n_dp, piece, LANES), F32),
             pltpu.VMEM((4, rows, LANES), F32),
             pltpu.VMEM((4, n_dp, piece, LANES), F32),
             pltpu.VMEM((rows, LANES), F32),
             pltpu.VMEM((2, rows, LANES), F32),
             pltpu.VMEM((n_dp, 1, LANES), F32),
-            pltpu.VMEM((n_dp, 1, LANES), F32),
+            pltpu.VMEM((n_y, NZ, 1, LANES), F32),
+            pltpu.VMEM((n_y, NZ, 1, LANES), F32),
             pltpu.VMEM((8, LANES), F32),
             pltpu.VMEM((NZ, 8, LANES), F32),
             pltpu.VMEM((n_y, 8, LANES), F32),
             pltpu.VMEM((n_group, 8, LANES), F32),
             dma((13,)),
-            dma((waves, n_dp)), dma((waves, n_dp)),
-            dma((n_dp,)), dma((n_dp,)),
+            dma((chunks, n_y)), dma((chunks, n_y)),
+            dma((chunks, NZ)), dma((chunks, NZ)),
+            dma((len(STRAIGHT), NZ)), dma((len(STRAIGHT), NZ)),
+            dma((n_y,)), dma((n_y,)),
+            dma((NZ,)), dma((NZ,)),
             dma((n_group,)), dma((n_group,)),
             dma((NZ,)), dma((NZ,)),
             dma((n_y,)), dma((n_y,)),
-            pltpu.SemaphoreType.REGULAR,
         ],
         compiler_params=pltpu.CompilerParams(
             collective_id=0, has_side_effects=True, vmem_limit_bytes=40 * 2**20
@@ -443,11 +490,11 @@
         )
     )
     return pl.pallas_call(
-        functools.partial(finish_kernel, (piece, span, width)),
+        functools.partial(finish_kernel, n_dp),
         out_shape=(result, result),
         in_specs=[vmem] * 5,
         out_specs=(hbm, hbm),
-        scratch_shapes=[pltpu.VMEM((rows, width), BF16), dma((12,))],
+        scratch_shapes=[pltpu.VMEM((rows, half), BF16), dma((12,))],
         compiler_params=pltpu.CompilerParams(vmem_limit_bytes=16 * 2**20),
         name="finish",
     )(*parts)

time: 110 us -> 107 us (0.973)
  Pallas kernels: 109 us -> 106 us
    pallas_call x2, Pallas kernels: 109 us -> 106 us  [the longest x1 104 us: local(): pl.pallas_call(functools.partial(kernel, (n_dp, n_group, piece, span)), o...]
where the time goes in v4:
time: 107 us
  Pallas kernels  106 us (99%)
    pallas_call x1, Pallas kernels, local(): pl.pallas_call(functools.partial(kernel, (n_dp, n_group, piece, span)), o...  104 us

profile of v4, /device:TPU:1, one launch (start us, length us, event | category | flops | bytes accessed | tf_op | source)
XLA Modules:
  0.0 106.7 jit_solution(9597428463654382863)
XLA Ops:
  0.6 103.9 %reshuffle.1 = (bf16[256,4096]{1,0:T(8,128)(2,1)S(1)}, bf16[256,2048]{1,0:T(8,128)(2,1)S(1)}, bf16[4,8,8,2048]{3,2,1,0:T(8,128)(2,1)S(1)}, bf16[2,128,128]{2,1,0:T(8,128)(2,1)S(1)}, f32[3,256,128]{2,1,0:T(8,128)S(1)}) custom-call(s32[1,32]{1,0:T(1,128)} %dest_hbm.1, s32[2,128]{1,0:T(2,128)} %bitcast.7, f32[2,128]{1,0:T(2,128)} %bitcast.8, s32[2,128]{1,0:T(2,128)} %bitcast.9, ...), custom_call_target="tpu_custom_call" | custom-call | tf_op jit(solution)/shard_map/reshuffle/pallas_call | solution.py:426
  104.6 2.1 %finish.1 = (bf16[256,4096]{1,0:T(8,128)(2,1)}, bf16[256,4096]{1,0:T(8,128)(2,1)}) custom-call(bf16[256,4096]{1,0:T(8,128)(2,1)S(1)} %get-tuple-element.7.white_r, bf16[256,2048]{1,0:T(8,128)(2,1)S(1)} %get-tuple-element.8.white_a, bf16[4,8,8,2048]{3,2,1,0:T(8,128)(2,1)S(1)} %get-tuple-element.9.last, bf16[2,128,128]{2,1,0:T(8,128)(2,1)S(1)} %get-tuple-element.10.chooser, ...), custom_call_target="tpu_custom_call" | custom-call | tf_op jit(solution)/shard_map/finish/pallas_call | solution.py:492

commit v5 on v4

--- a/solution.py
+++ b/solution.py
@@ -16,6 +16,7 @@
 CHUNKS = ((0, 0, 1), (0, 1, 1), (0, 2, 2), (1, 0, 2), (1, 2, 2))
 STRAIGHT = ((0, 0, 4), (1, 0, 2), (1, 2, 2))
 STEPS = (4, 3, 5, 2, 6, 1, 7)
+PLANES = (0, 1, 2, 3, 7, 4, 6, 5)
 
 
 def dot(a, b, dims=(((1,), (0,)), ((), ())), precision=None):
@@ -175,8 +176,16 @@
     def forward(w):
         for j in range(1, n_y):
             y_leg(w, j).wait_recv()
-        for k in STEPS:
-            z_leg(w, k).start()
+        if w == final:
+            for place in PLANES:
+                k = lax.rem(place - z + NZ, NZ)
+
+                @pl.when(k != 0)
+                def _():
+                    z_leg(w, k).start()
+        else:
+            for k in STEPS:
+                z_leg(w, k).start()
         q, first, width = CHUNKS[w]
         for j in range(1, n_y):
             if w == final:
@@ -336,14 +345,14 @@
     def advantage_straight():
         start_straight(1)
         start_straight(2)
+        forward(3)
 
     exchange(
         st_z, z, NZ, lambda k: {"dp": y * NZ + along_z(k)}, z_send, z_recv, advantage_straight
     )
     exchange(
-        st_y, y, n_y, lambda k: {"dp": along_y(k) * NZ + z}, y_send, y_recv, lambda: forward(3)
+        st_y, y, n_y, lambda k: {"dp": along_y(k) * NZ + z}, y_send, y_recv, lambda: forward(final)
     )
-    forward(final)
 
     total = part[...]
     count = jnp.maximum(total[0:1], 1.0)

time: 107 us -> 105 us (0.981)
  the two profiles are of different devices: /device:TPU:1 before, /device:TPU:72 now
where the time goes in v5:
time: 105 us
  Pallas kernels  105 us (100%)
    pallas_call x1, Pallas kernels, local(): pl.pallas_call(functools.partial(kernel, (n_dp, n_group, piece, span)), o...  102 us
    pallas_call x1, Pallas kernels, local(): pl.pallas_call(functools.partial(finish_kernel, n_dp), out_shape=(result,...  2.13 us

profile of v5, /device:TPU:72, one launch (start us, length us, event | category | flops | bytes accessed | tf_op | source)
XLA Modules:
  0.0 105.2 jit_solution(9486776393259576198)
XLA Ops:
  0.6 102.5 %reshuffle.1 = (bf16[256,4096]{1,0:T(8,128)(2,1)S(1)}, bf16[256,2048]{1,0:T(8,128)(2,1)S(1)}, bf16[4,8,8,2048]{3,2,1,0:T(8,128)(2,1)S(1)}, bf16[2,128,128]{2,1,0:T(8,128)(2,1)S(1)}, f32[3,256,128]{2,1,0:T(8,128)S(1)}) custom-call(s32[1,32]{1,0:T(1,128)} %dest_hbm.1, s32[2,128]{1,0:T(2,128)} %bitcast.7, f32[2,128]{1,0:T(2,128)} %bitcast.8, s32[2,128]{1,0:T(2,128)} %bitcast.9, ...), custom_call_target="tpu_custom_call" | custom-call | tf_op jit(solution)/shard_map/reshuffle/pallas_call | solution.py:435
  103.1 2.1 %finish.1 = (bf16[256,4096]{1,0:T(8,128)(2,1)}, bf16[256,4096]{1,0:T(8,128)(2,1)}) custom-call(bf16[256,4096]{1,0:T(8,128)(2,1)S(1)} %get-tuple-element.7.white_r, bf16[256,2048]{1,0:T(8,128)(2,1)S(1)} %get-tuple-element.8.white_a, bf16[4,8,8,2048]{3,2,1,0:T(8,128)(2,1)S(1)} %get-tuple-element.9.last, bf16[2,128,128]{2,1,0:T(8,128)(2,1)S(1)} %get-tuple-element.10.chooser, ...), custom_call_target="tpu_custom_call" | custom-call | tf_op jit(solution)/shard_map/finish/pallas_call | solution.py:501

commit v6 on v5

--- a/solution.py
+++ b/solution.py
@@ -358,7 +358,7 @@
     count = jnp.maximum(total[0:1], 1.0)
     for q in range(2):
         mean = total[1 + q : 2 + q] / count
-        spread = total[3 + q : 4 + q] / count - mean * mean
+        spread = jnp.maximum(total[3 + q : 4 + q] / count - mean * mean, 0.0)
         for s, value in enumerate((mean, lax.rsqrt(spread + 1e-05))):
             picked = jnp.sum(member[...] * value, axis=1, keepdims=True)
             (stats_r, stats)[q][s] = jnp.broadcast_to(picked, (rows, LANES))

time: 105 us -> 105 us (level)
  no operation moved by 1% of the time
where the time goes in v6:
time: 105 us
  Pallas kernels  105 us (100%)
    pallas_call x1, Pallas kernels, local(): pl.pallas_call(functools.partial(kernel, (n_dp, n_group, piece, span)), o...  102 us
    pallas_call x1, Pallas kernels, local(): pl.pallas_call(functools.partial(finish_kernel, n_dp), out_shape=(result,...  2.13 us

profile of v6, /device:TPU:72, one launch (start us, length us, event | category | flops | bytes accessed | tf_op | source)
XLA Modules:
  0.0 105.2 jit_solution(295612545674581085)
XLA Ops:
  0.6 102.5 %reshuffle.1 = (bf16[256,4096]{1,0:T(8,128)(2,1)S(1)}, bf16[256,2048]{1,0:T(8,128)(2,1)S(1)}, bf16[4,8,8,2048]{3,2,1,0:T(8,128)(2,1)S(1)}, bf16[2,128,128]{2,1,0:T(8,128)(2,1)S(1)}, f32[3,256,128]{2,1,0:T(8,128)S(1)}) custom-call(s32[1,32]{1,0:T(1,128)} %dest_hbm.1, s32[2,128]{1,0:T(2,128)} %bitcast.7, f32[2,128]{1,0:T(2,128)} %bitcast.8, s32[2,128]{1,0:T(2,128)} %bitcast.9, ...), custom_call_target="tpu_custom_call" | custom-call | tf_op jit(solution)/shard_map/reshuffle/pallas_call | solution.py:435
  103.1 2.1 %finish.1 = (bf16[256,4096]{1,0:T(8,128)(2,1)}, bf16[256,4096]{1,0:T(8,128)(2,1)}) custom-call(bf16[256,4096]{1,0:T(8,128)(2,1)S(1)} %get-tuple-element.7.white_r, bf16[256,2048]{1,0:T(8,128)(2,1)S(1)} %get-tuple-element.8.white_a, bf16[4,8,8,2048]{3,2,1,0:T(8,128)(2,1)S(1)} %get-tuple-element.9.last, bf16[2,128,128]{2,1,0:T(8,128)(2,1)S(1)} %get-tuple-element.10.chooser, ...), custom_call_target="tpu_custom_call" | custom-call | tf_op jit(solution)/shard_map/finish/pallas_call | solution.py:501

commit v7 on v6

--- a/solution.py
+++ b/solution.py
@@ -365,6 +365,10 @@
 
     tile = 256
     for w, (q, first, width) in enumerate(CHUNKS):
+        if w == final:
+            for c in range(len(CHUNKS)):
+                for j in range(1, n_y):
+                    y_leg(c, j).wait_send()
         for p, (kind, begin, _) in enumerate(STRAIGHT):
             if (kind, begin) == (q, first):
                 for k in STEPS:
@@ -386,9 +390,6 @@
             return c
 
         lax.fori_loop(0, width * unit // tile, finish, 0)
-    for w in range(len(CHUNKS)):
-        for j in range(1, n_y):
-            y_leg(w, j).wait_send()
 
 
 def finish_kernel(n_dp, white_r, white_a, last, chooser, stats, out_r, out_a, white, sem):

time: 105 us -> 105 us (level)
  no operation moved by 1% of the time
where the time goes in v7:
time: 105 us
  Pallas kernels  105 us (100%)
    pallas_call x1, Pallas kernels, local(): pl.pallas_call(functools.partial(kernel, (n_dp, n_group, piece, span)), o...  102 us
    pallas_call x1, Pallas kernels, local(): pl.pallas_call(functools.partial(finish_kernel, n_dp), out_shape=(result,...  2.13 us

profile of v7, /device:TPU:72, one launch (start us, length us, event | category | flops | bytes accessed | tf_op | source)
XLA Modules:
  0.0 105.2 jit_solution(14451519587570919058)
XLA Ops:
  0.6 102.4 %reshuffle.1 = (bf16[256,4096]{1,0:T(8,128)(2,1)S(1)}, bf16[256,2048]{1,0:T(8,128)(2,1)S(1)}, bf16[4,8,8,2048]{3,2,1,0:T(8,128)(2,1)S(1)}, bf16[2,128,128]{2,1,0:T(8,128)(2,1)S(1)}, f32[3,256,128]{2,1,0:T(8,128)S(1)}) custom-call(s32[1,32]{1,0:T(1,128)} %dest_hbm.1, s32[2,128]{1,0:T(2,128)} %bitcast.7, f32[2,128]{1,0:T(2,128)} %bitcast.8, s32[2,128]{1,0:T(2,128)} %bitcast.9, ...), custom_call_target="tpu_custom_call" | custom-call | tf_op jit(solution)/shard_map/reshuffle/pallas_call | solution.py:436
  103.1 2.1 %finish.1 = (bf16[256,4096]{1,0:T(8,128)(2,1)}, bf16[256,4096]{1,0:T(8,128)(2,1)}) custom-call(bf16[256,4096]{1,0:T(8,128)(2,1)S(1)} %get-tuple-element.7.white_r, bf16[256,2048]{1,0:T(8,128)(2,1)S(1)} %get-tuple-element.8.white_a, bf16[4,8,8,2048]{3,2,1,0:T(8,128)(2,1)S(1)} %get-tuple-element.9.last, bf16[2,128,128]{2,1,0:T(8,128)(2,1)S(1)} %get-tuple-element.10.chooser, ...), custom_call_target="tpu_custom_call" | custom-call | tf_op jit(solution)/shard_map/finish/pallas_call | solution.py:502
